TPU v7x, 128 devices: a whole 4x4x4 slice. The times are simulated.
128 devices in a mesh: rep: 1, dp: 128 (over x, y, z, core).
Axes of the slice: x: 4, y: 4, z: 4, core: 2. Of those that a mesh axis runs over, the one named last changes fastest.
Arguments:
- g_w_gate: bfloat16 [128, 2, 768, 1792], P(('rep', 'dp'))
- g_w_up: bfloat16 [128, 2, 768, 1792], P(('rep', 'dp'))
- g_w_down: bfloat16 [128, 2, 1792, 768], P(('rep', 'dp'))
- w_gate: bfloat16 [2, 768, 1792], replicated
- w_up: bfloat16 [2, 768, 1792], replicated
- w_down: bfloat16 [2, 1792, 768], replicated
- m_w_gate: float32 [2, 768, 1792], P(None, 'dp')
- m_w_up: float32 [2, 768, 1792], P(None, 'dp')
- m_w_down: float32 [2, 1792, 768], P(None, 'dp')
- v_w_gate: float32 [2, 768, 1792], P(None, 'dp')
- v_w_up: float32 [2, 768, 1792], P(None, 'dp')
- v_w_down: float32 [2, 1792, 768], P(None, 'dp')
Outputs:
- output 1: bfloat16 [2, 768, 1792], P('rep')
- output 2: bfloat16 [2, 768, 1792], P('rep')
- output 3: bfloat16 [2, 1792, 768], P('rep')
- output 4: float32 [2, 768, 1792], P('rep', 'dp')
- output 5: float32 [2, 768, 1792], P('rep', 'dp')
- output 6: float32 [2, 1792, 768], P('rep', 'dp')
- output 7: float32 [2, 768, 1792], P('rep', 'dp')
- output 8: float32 [2, 768, 1792], P('rep', 'dp')
- output 9: float32 [2, 1792, 768], P('rep', 'dp')
All inputs are finite; a program needn't handle non-finite values.
Results may differ from a plain program's by a relative error of at most 0.022.
Values are sent between devices in bfloat16 or wider.
A program may use at most 1.5 GiB of HBM per device.

v0:
```python
import jax
import jax.numpy as jnp
from jax import lax
from jax.sharding import PartitionSpec as P


def adamw(w, m, v, g):
    m = 0.9 * m + 0.1 * g
    v = 0.95 * v + 0.05 * g * g
    step = m * lax.rsqrt(v + 1e-8) + 0.1 * w
    return (w - 0.02 * step).astype(jnp.bfloat16), m, v


def solution(mesh):
    def step(*arrays):
        terms, weights, m, v = (arrays[i : i + 3] for i in (0, 3, 6, 9))
        gradients = [lax.psum_scatter(t[0], "dp", scatter_dimension=1, tiled=True).astype(jnp.float32) for t in terms]
        me = lax.axis_index("dp")
        own = [lax.dynamic_slice_in_dim(w, me * one.shape[1], one.shape[1], 1).astype(jnp.float32) for w, one in zip(weights, m, strict=True)]
        new = [adamw(w, m, v, g) for w, m, v, g in zip(own, m, v, gradients, strict=True)]
        whole = [lax.all_gather(one[0], "dp", axis=1, tiled=True) for one in new]
        return (*whole, *(one[1] for one in new), *(one[2] for one in new))

    all_of, cut = P(None, None, None), P(None, "dp", None)
    return jax.shard_map(
        step,
        mesh=mesh,
        in_specs=(P(("rep", "dp"), None, None, None),) * 3 + (all_of,) * 3 + (cut,) * 6,
        out_specs=(P("rep", None, None),) * 3 + (P("rep", "dp", None),) * 6,
        check_vma=False,
    )
```

profile of v0, /device:TPU:1, one launch (start us, length us, event | category | flops | bytes accessed | tf_op | source)
XLA Modules:
  0.0 500.0 jit_solution(13960679277745739571)
XLA Ops:
  7.2 0.0 all-reduce.6.cloned.1.call-start
  7.2 25.7 %copy.48 = bf16[1,2,1792,768]{3,1,2,0:T(2,128)(2,1)} copy(bf16[1,2,1792,768]{3,2,1,0:T(8,128)(2,1)} %param.14) | data formatting | bytes 11010048 | tf_op args[2]
  32.9 28.9 %copy_bitcast_fusion.1 = (bf16[2,768,1792]{2,0,1:T(2,128)(2,1)}, bf16[2,768,1792]{2,0,1:T(2,128)(2,1)}) fusion(bf16[1,2,768,1792]{3,2,1,0:T(8,128)(2,1)S(1)} %copy-done, bf16[1,2,768,1792]{3,2,1,0:T(8,128)(2,1)S(1)} %copy-done.1), kind=kLoop, calls=%fused_computation.1 | loop fusion | bytes 22020096 | tf_op jit(solution)/shard_map/squeeze | solution.py:17
  61.9 0.0 copy-start.6
  61.9 0.0 copy-start.7
  61.9 0.0 all-reduce.6.cloned.1.call-update
  62.0 0.0 all-gather.6.cloned.1.call-start
  62.0 1.1 constant_dynamic-slice_fusion.1
  63.1 218.8 %all-reduce.6.cloned.1.call-done = (bf16[2,768,1792]{2,0,1:T(2,128)(2,1)}, bf16[2,768,1792]{2,0,1:T(2,128)(2,1)}, bf16[2,1792,768]{2,0,1:T(2,128)(2,1)}) async-done(((bf16[2,768,1792]{2,0,1:T(2,128)(2,1)}, bf16[2,768,1792]{2,0,1:T(2,128)(2,1)}, bf16[2,1792,768]{2,0,1:T(2,128)(2,1)}), (bf16[2,768,1792]{2,0,1:T(2,128)(2,1)}, bf16[2,768,1792]{2,0,1:T(2,128)(2,1)}, ...) | async-done | bytes 16515088
  281.9 1.7 fusion.13
  283.6 0.0 all-gather.6.cloned.1.call-update
  283.6 0.0 all-gather.4.cloned.1.call-start
  283.7 1.7 fusion.12
  285.4 0.0 all-gather.4.cloned.1.call-update
  285.4 0.0 all-gather.8.cloned.1.call-start
  285.4 0.9 constant_dynamic-slice_fusion
  286.4 1.7 fusion.14
  288.1 0.0 all-gather.8.cloned.1.call-update
  288.1 63.2 %all-gather.6.cloned.1.call-done = bf16[2,768,1792]{2,0,1:T(2,128)(2,1)} async-done(((bf16[2,6,1792]{2,0,1:T(2,128)(2,1)}), bf16[2,768,1792]{2,0,1:T(2,128)(2,1)}) %all-gather.6.cloned.1.call-update) | async-done | bytes 5505040 | tf_op jit(solution)/shard_map/all_gather | solution.py:21
  351.2 5.7 %copy.37 = bf16[2,768,1792]{2,1,0:T(8,128)(2,1)} copy(bf16[2,768,1792]{2,0,1:T(2,128)(2,1)} %all-gather.6.cloned.1.call-done) | data formatting | bytes 11010048
  356.9 62.9 %all-gather.4.cloned.1.call-done = bf16[2,768,1792]{2,0,1:T(2,128)(2,1)} async-done(((bf16[2,6,1792]{2,0,1:T(2,128)(2,1)}), bf16[2,768,1792]{2,0,1:T(2,128)(2,1)}) %all-gather.4.cloned.1.call-update) | async-done | bytes 5505040 | tf_op jit(solution)/shard_map/all_gather | solution.py:21
  419.9 5.7 %copy.36 = bf16[2,768,1792]{2,1,0:T(8,128)(2,1)} copy(bf16[2,768,1792]{2,0,1:T(2,128)(2,1)} %all-gather.4.cloned.1.call-done) | data formatting | bytes 11010048
  425.5 62.2 %all-gather.8.cloned.1.call-done = bf16[2,1792,768]{2,0,1:T(2,128)(2,1)} async-done(((bf16[2,14,768]{2,0,1:T(2,128)(2,1)}), bf16[2,1792,768]{2,0,1:T(2,128)(2,1)}) %all-gather.8.cloned.1.call-update) | async-done | bytes 5505040 | tf_op jit(solution)/shard_map/all_gather | solution.py:21
  487.8 5.7 %copy.38 = bf16[2,1792,768]{2,1,0:T(8,128)(2,1)} copy(bf16[2,1792,768]{2,0,1:T(2,128)(2,1)} %all-gather.8.cloned.1.call-done) | data formatting | bytes 11010048
  (14 shorter events, 0.0 us)
Async XLA Ops:
  7.2 274.7 %all-reduce.6.cloned.1.call-start = ((), (), s32[]{:S(2)}) async-start(), calls=%async_computation.3 | async-start | bytes 33030144
  7.2 25.7 %copy-start = (bf16[1,2,768,1792]{3,2,1,0:T(8,128)(2,1)S(1)}, bf16[1,2,768,1792]{3,2,1,0:T(8,128)(2,1)}, u32[]{:S(2)}) copy-start(bf16[1,2,768,1792]{3,2,1,0:T(8,128)(2,1)} %param.13) | copy-start | bytes 16515076
  7.2 25.7 %copy-start.1 = (bf16[1,2,768,1792]{3,2,1,0:T(8,128)(2,1)S(1)}, bf16[1,2,768,1792]{3,2,1,0:T(8,128)(2,1)}, u32[]{:S(2)}) copy-start(bf16[1,2,768,1792]{3,2,1,0:T(8,128)(2,1)} %param.12) | copy-start | bytes 16515076
  61.9 220.0 %copy-start.2 = (f32[2,6,1792]{2,0,1:T(2,128)S(1)}, f32[2,6,1792]{2,0,1:T(2,128)}, u32[]{:S(2)}) copy-start(f32[2,6,1792]{2,0,1:T(2,128)} %param.22) | copy-start | bytes 258052
  61.9 220.0 %copy-start.3 = (f32[2,6,1792]{2,0,1:T(2,128)S(1)}, f32[2,6,1792]{2,0,1:T(2,128)}, u32[]{:S(2)}) copy-start(f32[2,6,1792]{2,0,1:T(2,128)} %param.19) | copy-start | bytes 258052
  61.9 221.8 %copy-start.4 = (f32[2,6,1792]{2,0,1:T(2,128)S(1)}, f32[2,6,1792]{2,0,1:T(2,128)}, u32[]{:S(2)}) copy-start(f32[2,6,1792]{2,0,1:T(2,128)} %param.21) | copy-start | bytes 258052
  61.9 221.8 %copy-start.5 = (f32[2,6,1792]{2,0,1:T(2,128)S(1)}, f32[2,6,1792]{2,0,1:T(2,128)}, u32[]{:S(2)}) copy-start(f32[2,6,1792]{2,0,1:T(2,128)} %param.18) | copy-start | bytes 258052
  61.9 224.4 %copy-start.6 = (f32[2,14,768]{2,0,1:T(2,128)S(1)}, f32[2,14,768]{2,0,1:T(2,128)}, u32[]{:S(2)}) copy-start(f32[2,14,768]{2,0,1:T(2,128)} %param.23) | copy-start | bytes 258052
  61.9 224.4 %copy-start.7 = (f32[2,14,768]{2,0,1:T(2,128)S(1)}, f32[2,14,768]{2,0,1:T(2,128)}, u32[]{:S(2)}) copy-start(f32[2,14,768]{2,0,1:T(2,128)} %param.20) | copy-start | bytes 258052
  62.0 289.3 %all-gather.6.cloned.1.call-start = ((), (), s32[]{:S(2)}) async-start(), calls=%async_computation.1 | async-start | bytes 5548032 | tf_op jit(solution)/shard_map/all_gather | solution.py:21
  283.6 136.3 %all-gather.4.cloned.1.call-start = ((), (), s32[]{:S(2)}) async-start(), calls=%async_computation | async-start | bytes 5548032 | tf_op jit(solution)/shard_map/all_gather | solution.py:21
  285.4 202.4 %all-gather.8.cloned.1.call-start = ((), (), s32[]{:S(2)}) async-start(), calls=%async_computation.2 | async-start | bytes 5548032 | tf_op jit(solution)/shard_map/all_gather | solution.py:21
Sparse Core Ops, SparseCore 0:
  62.1 219.7 all-reduce.5
  285.3 65.8 all-gather.5
  354.7 65.1 all-gather.3
  422.6 65.1 all-gather.7
where the time goes:
time: 500 us
  waiting for transfers between devices  407 us (81%)
  local copies, waits for them, and re-layouts  73.8 us (15%)
  between operations  13.9 us (3%)
  other arithmetic  5.04 us (1%)
    unnamed x5, waiting for transfers between devices  219 us
    all_gather x3, waiting for transfers between devices, step(): whole = [lax.all_gather(one[0], 'dp', axis=1, tiled=True) for one in new]  188 us
    unnamed x20, local copies, waits for them, and re-layouts  42.8 us
    squeeze x1, local copies, waits for them, and re-layouts, step(): t[0]  28.9 us
  transfers between devices with their start and end apart: 4, of which 4 were waited for; matrix products, arithmetic and copies ran while one was open for 3% of the time, Pallas kernels for 0%

commit v1 on v0

v1 whole, which is shorter than its diff:
```python
import jax
import jax.numpy as jnp
from jax import lax
from jax.experimental import pallas as pl
from jax.experimental.pallas import tpu as pltpu
from jax.sharding import PartitionSpec as P

MESH = pl.DeviceIdType.MESH
BF, F32 = jnp.bfloat16, jnp.float32

COLS = (1792, 1792, 768)
R = (48, 48, 112)
RC = (12, 12, 28)
RP = (16, 16, 32)
H = (6, 6, 14)
AXES = ((0, 1, 2), (1, 2, 0), (2, 0, 1))
TILES = ((2, 2, 3), (2, 2, 3), (1, 1, 1))
CHUNKS = len(TILES[0])
MSGS = 25
WHEN = (0, 4, 8, 12, 15, 18, 20, 22, 24, 26, 28, 31, 34, 37, 42, 47, 55)
LAG = 8


def adamw(w, m, v, g):
    m = 0.9 * m + 0.1 * g
    v = 0.95 * v + 0.05 * g * g
    step = m * lax.rsqrt(v + 1e-8) + 0.1 * w
    return (w - 0.02 * step).astype(BF), m, v


class Unit:
    def __init__(self, color, chunk, way, c0, cn, uid):
        self.a, self.chunk, self.s, self.c0, self.cn, self.u = color, chunk, way, c0, cn, uid
        self.cols = pl.ds(c0, cn)


def units():
    found, uid = [], 0
    for a in range(3):
        c0 = 0
        for k, t in enumerate(TILES[a]):
            for way in (1, -1):
                found.append(Unit(a, k, way, c0, 128 * t, uid))
                c0 += 128 * t
                uid += 1
        assert c0 == COLS[a]
    return found


def comm_kernel(*refs):
    it = iter(refs)

    def take(n):
        return [next(it) for _ in range(n)]

    g, w, m, v = take(3), take(3), take(3), take(3)
    out, gfin = take(3), take(3)
    own, part = take(3), take(3)
    psum = next(it)
    s1, r1, a1, s2, r2, a2, s3, r3 = (take(3) for _ in range(8))
    gs, gr, wx, ws, ag3 = (take(3) for _ in range(5))
    ag2u, tmp, osem, ssem, rsem = take(5)
    all_units = units()

    me = lax.axis_index("dp")
    rep = lax.axis_index("rep")
    c = lax.rem(me, 2)
    pos = (me // 32, lax.rem(me // 8, 4), lax.rem(me // 2, 4))
    strides = (32, 8, 2)
    partner = me + 1 - 2 * c

    def near(axis, d):
        return me + (lax.rem(pos[axis] + d + 4, 4) - pos[axis]) * strides[axis]

    def send(u, i, src, dst, to):
        pltpu.make_async_remote_copy(
            src_ref=src, dst_ref=dst, send_sem=ssem.at[u.u, i], recv_sem=rsem.at[u.u, i], device_id=(rep, to), device_id_type=MESH
        ).start()

    def waiter(u, i, ref):
        return pltpu.make_async_remote_copy(
            src_ref=ref, dst_ref=ref, send_sem=ssem.at[u.u, i], recv_sem=rsem.at[u.u, i], device_id=(rep, partner), device_id_type=MESH
        )

    pending = []

    def post(u, i, src, dst, to):
        send(u, i, src, dst, to)
        pending.append((u, i, src))

    def got(u, i, ref):
        waiter(u, i, ref).wait_recv()

    def loads(u):
        return pltpu.make_async_copy(g[u.a].at[c, :, :, :, u.cols], own[u.a].at[:, :, :, u.cols], osem.at[u.u])

    def mine1(u, q, i):
        if u.a == 2:
            return psum[q, i, :, u.cols]
        at = (q, i) if u.a == 0 else (i, q)
        return own[u.a][(*at, slice(None), u.cols)].astype(F32) + part[u.a][(*at, slice(None), u.cols)].astype(F32)

    def axis(u, phase):
        return AXES[u.a][phase]

    def at(u, phase, d):
        return lax.rem(pos[axis(u, phase)] + d + 4, 4)

    S = slice(None)

    def sum1(u, i, q, came):
        @pl.loop(0, 4)
        def _(j):
            x = mine1(u, q, j)
            if came:
                x = x + r1[u.a][0, j, :, u.cols].astype(F32)
            s1[u.a][i, j, :, u.cols] = x.astype(BF)

        post(u, i, s1[u.a].at[i, :, :, u.cols], r1[u.a].at[i, :, :, u.cols], near(axis(u, 0), -u.s if i == 1 else u.s))

    def sum2(u, i, q, came):
        x = a1[u.a][q, :, u.cols]
        if came:
            x = x + r2[u.a][0, :, u.cols].astype(F32)
        s2[u.a][i, :, u.cols] = x.astype(BF)
        post(u, 3 + i, s2[u.a].at[i, :, u.cols], r2[u.a].at[i, :, u.cols], near(axis(u, 1), -u.s if i == 1 else u.s))

    def sum3(u, i, q, came):
        x = a2[u.a][q, :, u.cols]
        if came:
            x = x + r3[u.a][0, :, u.cols].astype(F32)
        s3[u.a][i, :, u.cols] = x.astype(BF)
        post(u, 6 + i, s3[u.a].at[i, :, u.cols], r3[u.a].at[i, :, u.cols], near(axis(u, 2), -u.s if i == 1 else u.s))

    def start_sum(u, phase, fn):
        fn(u, 0, at(u, phase, 2), False)
        fn(u, 1, at(u, phase, -u.s), False)

    def each(k):
        return [u for u in all_units if u.chunk == k]

    def st0(k):
        for u in each(k):
            post(u, 20, g[u.a].at[1 - c, :, :, :, u.cols], part[u.a].at[:, :, :, u.cols], partner)

    def st1(k):
        for u in each(k):
            loads(u).wait()
            got(u, 20, part[u.a].at[:, :, :, u.cols])
            if u.a == 2:

                @pl.loop(0, 4)
                def _(x):
                    for y in range(4):
                        t = own[2][x, y, :, u.cols].astype(F32) + part[2][x, y, :, u.cols].astype(F32)
                        for z in range(4):
                            psum[z, x, 28 * y : 28 * y + 28, u.cols] = t[28 * z : 28 * z + 28]

            sum1(u, 0, at(u, 0, 2), False)
        for u in each(k):
            sum1(u, 1, at(u, 0, -u.s), False)

    def st2(k):
        for u in each(k):
            got(u, 0, r1[u.a].at[0, :, :, u.cols])
            sum1(u, 2, at(u, 0, u.s), True)

    def st3(k):
        for u in each(k):
            got(u, 1, r1[u.a].at[1, :, :, u.cols])
            got(u, 2, r1[u.a].at[2, :, :, u.cols])
            q = pos[axis(u, 0)]

            def total(j):
                return mine1(u, q, j) + r1[u.a][1, j, :, u.cols].astype(F32) + r1[u.a][2, j, :, u.cols].astype(F32)

            if u.a == 1:
                for j in range(4):
                    t = total(j)
                    for z in range(4):
                        a1[1][z, 12 * j : 12 * j + 12, u.cols] = t[12 * z : 12 * z + 12]
            else:

                @pl.loop(0, 4)
                def _(j):
                    a1[u.a][j, :, u.cols] = total(j)

            sum2(u, 0, at(u, 1, 2), False)
        for u in each(k):
            sum2(u, 1, at(u, 1, -u.s), False)

    def st4(k):
        for u in each(k):
            got(u, 3, r2[u.a].at[0, :, u.cols])
            sum2(u, 2, at(u, 1, u.s), True)

    def st5(k):
        for u in each(k):
            got(u, 4, r2[u.a].at[1, :, u.cols])
            got(u, 5, r2[u.a].at[2, :, u.cols])
            rc = RC[u.a]
            t = a1[u.a][pos[axis(u, 1)], :, u.cols] + r2[u.a][1, :, u.cols].astype(F32) + r2[u.a][2, :, u.cols].astype(F32)
            for q in range(4):
                a2[u.a][q, 0:rc, u.cols] = t[rc * q : rc * q + rc]
            sum3(u, 0, at(u, 2, 2), False)
        for u in each(k):
            sum3(u, 1, at(u, 2, -u.s), False)

    def st6(k):
        for u in each(k):
            got(u, 6, r3[u.a].at[0, :, u.cols])
            sum3(u, 2, at(u, 2, u.s), True)

    def st7(k):
        for u in each(k):
            got(u, 7, r3[u.a].at[1, :, u.cols])
            got(u, 8, r3[u.a].at[2, :, u.cols])
            h = H[u.a]
            t = a2[u.a][pos[axis(u, 2)], :, u.cols] + r3[u.a][1, :, u.cols].astype(F32) + r3[u.a][2, :, u.cols].astype(F32)
            for q in range(2):
                gs[u.a][q, 0:h, u.cols] = t[h * q : h * q + h].astype(BF)
            post(u, 9, gs[u.a].at[1 - c, :, u.cols], gr[u.a].at[:, u.cols], partner)

    def st8(k):
        for u in each(k):
            got(u, 9, gr[u.a].at[:, u.cols])
            h = H[u.a]
            for mine in (False, True):
                layer = c if mine else 1 - c
                grad = gs[u.a][c, 0:h, u.cols] if mine else gr[u.a][0:h, u.cols]
                grad = grad.astype(F32)
                gfin[u.a][layer, :, u.cols] = grad
                new, _, _ = adamw(w[u.a][layer, :, u.cols].astype(F32), m[u.a][layer, :, u.cols], v[u.a][layer, :, u.cols], grad)
                if mine:
                    wx[u.a][c, 0:h, u.cols] = new
                else:
                    ws[u.a][0:h, u.cols] = new
                    post(u, 10, ws[u.a].at[:, u.cols], wx[u.a].at[c, :, u.cols], partner)

    def spread(u, base, phase, i, ref, q):
        post(u, base + i, ref(q), ref(q), near(axis(u, phase), -u.s if i == 1 else u.s))

    def start_spread(u, base, phase, ref):
        q = pos[axis(u, phase)]
        spread(u, base, phase, 0, ref, q)
        spread(u, base, phase, 1, ref, q)

    def pass_on(u, base, phase, ref):
        q = at(u, phase, -u.s)
        got(u, base, ref(q))
        spread(u, base, phase, 2, ref, q)

    def end_spread(u, base, phase, ref):
        got(u, base + 1, ref(at(u, phase, u.s)))
        got(u, base + 2, ref(at(u, phase, 2)))

    def ref3(u):
        return lambda q: ag3[u.a].at[q, :, u.cols]

    def ref2(u):
        if u.a == 0:
            return lambda q: out[0].at[c, pos[0], q, :, u.cols]
        if u.a == 1:
            return lambda q: ag2u.at[q, :, u.cols]
        return lambda q: out[2].at[c, pos[2], q, :, u.cols]

    def ref1(u):
        if u.a == 1:
            return lambda q: out[1].at[c, :, q, :, u.cols]
        return lambda q: out[u.a].at[c, q, :, :, u.cols]

    def st9(k):
        for u in each(k):
            got(u, 10, wx[u.a].at[1 - c, :, u.cols])
            h, rp = H[u.a], RP[u.a]
            for q in range(2):
                tmp[h * q : h * q + h, 0 : u.cn] = wx[u.a][q, 0:h, u.cols].astype(F32)
            ag3[u.a][pos[axis(u, 2)], :, u.cols] = tmp[0:rp, 0 : u.cn].astype(BF)
            start_spread(u, 11, 2, ref3(u))

    def st10(k):
        for u in each(k):
            pass_on(u, 11, 2, ref3(u))

    def st11(k):
        for u in each(k):
            end_spread(u, 11, 2, ref3(u))
            rc, r = RC[u.a], R[u.a]
            for q in range(4):
                tmp[rc * q : rc * q + rc, 0 : u.cn] = ag3[u.a][q, 0:rc, u.cols].astype(F32)
            ref2(u)(pos[axis(u, 1)])[...] = tmp[0:r, 0 : u.cn].astype(BF)
            start_spread(u, 14, 1, ref2(u))

    def st12(k):
        for u in each(k):
            pass_on(u, 14, 1, ref2(u))

    def st13(k):
        for u in each(k):
            end_spread(u, 14, 1, ref2(u))
            if u.a == 1:
                for x in range(4):
                    for z in range(4):
                        tmp[12 * z : 12 * z + 12, 0 : u.cn] = ag2u[z, 12 * x : 12 * x + 12, u.cols].astype(F32)
                    out[1][c, x, pos[1], :, u.cols] = tmp[0:48, 0 : u.cn].astype(BF)
            start_spread(u, 17, 0, ref1(u))
            over(u, 21, pos[axis(u, 0)])

    def mate(u):
        if u.a == 1:
            return lambda q: out[1].at[1 - c, :, q, :, u.cols]
        return lambda q: out[u.a].at[1 - c, q, :, :, u.cols]

    def over(u, i, q):
        post(u, i, ref1(u)(q), ref1(u)(q), partner)

    def st14(k):
        for u in each(k):
            pass_on(u, 17, 0, ref1(u))
            over(u, 22, at(u, 0, -u.s))

    def st15(k):
        for u in each(k):
            got(u, 18, ref1(u)(at(u, 0, u.s)))
            over(u, 23, at(u, 0, u.s))
        for u in each(k):
            got(u, 19, ref1(u)(at(u, 0, 2)))
            over(u, 24, at(u, 0, 2))

    def st16(k):
        for u in each(k):
            other = mate(u)
            got(u, 21, other(pos[axis(u, 0)]))
            got(u, 22, other(at(u, 0, -u.s)))
            got(u, 23, other(at(u, 0, u.s)))
            got(u, 24, other(at(u, 0, 2)))

    for k in range(CHUNKS):
        for u in each(k):
            loads(u).start()
    barrier = pltpu.get_barrier_semaphore()
    peers = [partner] + [near(x, d) for x in range(3) for d in (1, -1)]
    for peer in peers:
        pl.semaphore_signal(barrier, inc=1, device_id=(rep, peer), device_id_type=MESH)
    pl.semaphore_wait(barrier, len(peers))

    stages = (st0, st1, st2, st3, st4, st5, st6, st7, st8, st9, st10, st11, st12, st13, st14, st15, st16)
    for k in range(CHUNKS):
        st0(k)
    order = sorted((WHEN[s] + LAG * k, k, s) for s in range(1, len(stages)) for k in range(CHUNKS))
    for _, k, s in order:
        stages[s](k)
    for u, i, src in pending:
        waiter(u, i, src).wait_send()


def finish_kernel(*refs):
    it = iter(refs)

    def take(n):
        return [next(it) for _ in range(n)]

    src, g, m, v = take(3), take(3), take(3), take(3)
    out, mo, vo = take(3), take(3), take(3)
    buf, tmp, sem, bsem = take(4)
    copies = [pltpu.make_async_copy(src[a], out[a], sem.at[a]) for a in range(2)]
    for one in copies:
        one.start()
    for a in range(3):
        grad = g[a][...]
        mo[a][...] = 0.9 * m[a][...] + 0.1 * grad
        vo[a][...] = 0.95 * v[a][...] + 0.05 * grad * grad

    def back(layer, x, n):
        return pltpu.make_async_copy(buf.at[n], out[2].at[layer, x], bsem.at[n])

    for layer in range(2):
        for x in range(4):
            n = 4 * layer + x

            @pl.loop(0, 3)
            def _(j):
                cols = pl.ds(pl.multiple_of(j * 256, 256), 256)
                for y in range(4):
                    for z in range(4):
                        tmp[28 * z : 28 * z + 28] = src[2][layer, z, x, 28 * y : 28 * y + 28, cols].astype(F32)
                    buf[n, y, :, cols] = tmp[...].astype(BF)

            back(layer, x, n).start()
    for layer in range(2):
        for x in range(4):
            back(layer, x, 4 * layer + x).wait()
    for one in copies:
        one.wait()


def solution(mesh):
    def step(*arrays):
        terms, weights, m, v = (arrays[i : i + 3] for i in (0, 3, 6, 9))
        me = lax.axis_index("dp")
        terms = [t[0].reshape(2, 4, 4, R[a], COLS[a]) for a, t in enumerate(terms)]
        own = [lax.dynamic_slice_in_dim(w, me * one.shape[1], one.shape[1], 1) for w, one in zip(weights, m, strict=True)]
        vmem = pl.BlockSpec(memory_space=pltpu.VMEM)
        hbm = pl.BlockSpec(memory_space=pl.ANY)
        per = lambda fn, dt: [pltpu.VMEM(fn(a), dt) for a in range(3)]
        whole = [(2, 4, 4, R[a], COLS[a]) for a in range(3)]
        n = len(units())
        scratch = (
            per(lambda a: (4, 4, R[a], COLS[a]), BF) * 2
            + [pltpu.VMEM((4, 4, R[2], COLS[2]), F32)]
            + per(lambda a: (3, 4, R[a], COLS[a]), BF) * 2
            + per(lambda a: (4, R[a], COLS[a]), F32)
            + per(lambda a: (3, R[a], COLS[a]), BF) * 2
            + per(lambda a: (4, RP[a], COLS[a]), F32)
            + per(lambda a: (3, RP[a], COLS[a]), BF) * 2
            + per(lambda a: (2, 16, COLS[a]), BF)
            + per(lambda a: (16, COLS[a]), BF)
            + per(lambda a: (2, 16, COLS[a]), BF)
            + per(lambda a: (16, COLS[a]), BF)
            + per(lambda a: (4, RP[a], COLS[a]), BF)
            + [pltpu.VMEM((4, 48, COLS[1]), BF), pltpu.VMEM((112, 128 * max(max(t) for t in TILES)), F32)]
            + [pltpu.SemaphoreType.DMA((n,)), pltpu.SemaphoreType.DMA((n, MSGS)), pltpu.SemaphoreType.DMA((n, MSGS))]
        )
        got = pl.pallas_call(
            comm_kernel,
            out_shape=[pltpu.VMEM(s, BF) for s in whole] + [jax.ShapeDtypeStruct((2, H[a], COLS[a]), F32) for a in range(3)],
            in_specs=[hbm] * 3 + [vmem] * 9,
            out_specs=[vmem] * 6,
            scratch_shapes=scratch,
            compiler_params=pltpu.CompilerParams(collective_id=0, has_side_effects=True, vmem_limit_bytes=48_500_000),
        )(*terms, *own, *m, *v)
        kept = [pltpu.with_memory_space_constraint(x, pltpu.VMEM) for x in got[:3]]
        shapes = [jax.ShapeDtypeStruct(s, BF) for s in whole] + [jax.ShapeDtypeStruct((2, H[a], COLS[a]), F32) for a in range(3)] * 2
        done = pl.pallas_call(
            finish_kernel,
            out_shape=shapes,
            in_specs=[vmem] * 12,
            out_specs=[hbm] * 3 + [vmem] * 6,
            scratch_shapes=[
                pltpu.VMEM((8, 4, R[2], COLS[2]), BF),
                pltpu.VMEM((112, 256), F32),
                pltpu.SemaphoreType.DMA((2,)),
                pltpu.SemaphoreType.DMA((8,)),
            ],
            compiler_params=pltpu.CompilerParams(vmem_limit_bytes=20_000_000),
        )(*kept, *got[3:], *m, *v)
        return [x.reshape(w.shape) for x, w in zip(done[:3], weights, strict=True)] + list(done[3:])

    def run(*arrays):
        return tuple(step(*arrays))

    all_of, cut = P(None, None, None), P(None, "dp", None)
    return jax.shard_map(
        run,
        mesh=mesh,
        in_specs=(P(("rep", "dp"), None, None, None),) * 3 + (all_of,) * 3 + (cut,) * 6,
        out_specs=(P("rep", None, None),) * 3 + (P("rep", "dp", None),) * 6,
        check_vma=False,
    )
```

time: 500 us -> 133 us (0.27)
  waiting for transfers between devices: 407 us -> 0 us
  Pallas kernels: 0 us -> 113 us
  local copies, waits for them, and re-layouts: 73.8 us -> 19.2 us
  between operations: 13.9 us -> 0.75 us
  other arithmetic: 5.04 us -> 0 us
    unnamed x5 -> x0, waiting for transfers between devices: 219 us -> none
    all_gather x3 -> x0, waiting for transfers between devices: 188 us -> none  [step(): whole = [lax.all_gather(one[0], 'dp', axis=1, tiled=True) for one in new]]
    pallas_call x0 -> x2, Pallas kernels: none -> 113 us  [the longest x1 107 us: step(): pl.pallas_call(comm_kernel, out_shape=[pltpu.VMEM(s, BF) for s in whole]...]
    squeeze x1 -> x0, local copies, waits for them, and re-layouts: 28.9 us -> none  [step(): t[0]]
    unnamed x20 -> x30, local copies, waits for them, and re-layouts: 42.8 us -> 16.1 us
    convert_element_type x3 -> x0, other arithmetic: 5.04 us -> none  [adamw(): return ((w - 0.02 * step).astype(jnp.bfloat16), m, v)]
  transfers between devices with their start and end apart: 4 -> 0, of which waited for: 4 -> 0; matrix products, arithmetic and copies ran while one was open for 3% -> 0% of each run, Pallas kernels for 0% -> 0%
where the time goes in v1:
time: 133 us
  Pallas kernels  113 us (85%)
  local copies, waits for them, and re-layouts  19.2 us (14%)
    pallas_call x1, Pallas kernels, step(): pl.pallas_call(comm_kernel, out_shape=[pltpu.VMEM(s, BF) for s in whole]...  107 us
    unnamed x30, local copies, waits for them, and re-layouts  16.1 us
    pallas_call x1, Pallas kernels, step(): pl.pallas_call(finish_kernel, out_shape=shapes, in_specs=[vmem] * 12, out...  5.86 us
    dynamic_slice x2, local copies, waits for them, and re-layouts, step(): lax.dynamic_slice_in_dim(w, me * one.shape[1], one.shape[1], 1)  3.16 us

profile of v1, /device:TPU:1, one launch (start us, length us, event | category | flops | bytes accessed | tf_op | source)
XLA Modules:
  0.0 132.5 jit_solution(6118069198117301105)
XLA Ops:
  0.6 1.5 %constant_dynamic-slice_fusion.refs_5_ = bf16[2,14,768]{2,1,0:T(8,128)(2,1)} fusion(bf16[2,1792,768]{2,1,0:T(8,128)(2,1)} %param.17, s32[]{:T(128)S(6)} %select_n.8), kind=kLoop, calls=%fused_computation | loop fusion | bytes 86020 | tf_op jit(solution)/shard_map/dynamic_slice | solution.py:402
  2.2 1.5 %copy.23.refs_8_ = f32[2,14,768]{2,1,0:T(8,128)} copy(f32[2,14,768]{2,0,1:T(2,128)} %param.20) | data formatting | bytes 172032 | tf_op args[8]
  3.7 1.5 %copy.26.refs_11_ = f32[2,14,768]{2,1,0:T(8,128)} copy(f32[2,14,768]{2,0,1:T(2,128)} %param.23) | data formatting | bytes 172032 | tf_op args[11]
  5.2 1.6 %constant_dynamic-slice_fusion.1 = (bf16[2,6,1792]{2,1,0:T(8,128)(2,1)}, bf16[2,6,1792]{2,1,0:T(8,128)(2,1)}) fusion(bf16[2,768,1792]{2,1,0:T(8,128)(2,1)} %param.16, s32[]{:T(128)S(6)} %select_n.7, bf16[2,768,1792]{2,1,0:T(8,128)(2,1)} %param.15), kind=kLoop, calls=%fused_computation.1 | loop fusion | bytes 172036 | tf_op jit(solution)/shard_map/dynamic_slice | solution.py:402
  6.9 1.5 %copy.21.refs_6_ = f32[2,6,1792]{2,1,0:T(8,128)} copy(f32[2,6,1792]{2,0,1:T(2,128)} %param.18) | data formatting | bytes 172032 | tf_op args[6]
  8.4 1.5 %copy.22.refs_7_ = f32[2,6,1792]{2,1,0:T(8,128)} copy(f32[2,6,1792]{2,0,1:T(2,128)} %param.19) | data formatting | bytes 172032 | tf_op args[7]
  10.0 1.5 %copy.24.refs_9_ = f32[2,6,1792]{2,1,0:T(8,128)} copy(f32[2,6,1792]{2,0,1:T(2,128)} %param.21) | data formatting | bytes 172032 | tf_op args[9]
  11.5 1.5 %copy.25.refs_10_ = f32[2,6,1792]{2,1,0:T(8,128)} copy(f32[2,6,1792]{2,0,1:T(2,128)} %param.22) | data formatting | bytes 172032 | tf_op args[10]
  13.1 0.0 copy-start.4
  13.1 0.0 copy-start.5
  13.1 106.7 %shard_map.187 = (bf16[2,4,4,48,1792]{4,3,2,1,0:T(8,128)(2,1)S(1)}, bf16[2,4,4,48,1792]{4,3,2,1,0:T(8,128)(2,1)S(1)}, bf16[2,4,4,112,768]{4,3,2,1,0:T(8,128)(2,1...) custom-call(bf16[2,4,4,48,1792]{4,3,2,1,0:T(8,128)(2,1)} %bitcast.6, ...), custom_call_target="tpu_custom_call" | custom-call | tf_op jit(solution)/shard_map/pallas_call | solution.py:424
  119.8 0.0 copy-done
  119.8 0.0 copy-done.1
  119.8 0.0 copy-done.2
  119.8 0.9 copy-done.6
  120.7 0.9 copy-done.7
  121.6 0.9 copy-done.8
  122.5 5.9 %shard_map.188 = (bf16[2,4,4,48,1792]{4,3,2,1,0:T(8,128)(2,1)}, bf16[2,4,4,48,1792]{4,3,2,1,0:T(8,128)(2,1)}, bf16[2,4,4,112,768]{4,3,2,1,0:T(8,128)(2,1)}, f32[...) custom-call(bf16[2,4,4,48,1792]{4,3,2,1,0:T(8,128)(2,1)S(1)} %get-tu, ...), custom_call_target="tpu_custom_call" | custom-call | tf_op jit(solution)/shard_map/pallas_call | solution.py:434
  128.4 0.7 copy.33
  129.1 0.7 copy.34
  129.7 0.7 copy.35
  130.4 0.7 copy.36
  131.1 0.7 copy.37
  131.8 0.7 copy.38
  (10 shorter events, 0.0 us)
Async XLA Ops:
  13.1 106.7 %copy-start = (f32[2,6,1792]{2,1,0:T(8,128)S(1)}, f32[2,6,1792]{2,1,0:T(8,128)}, u32[]{:S(2)}) copy-start(f32[2,6,1792]{2,1,0:T(8,128)} %copy.21.refs_6_) | copy-start | bytes 258052
  13.1 106.7 %copy-start.1 = (f32[2,6,1792]{2,1,0:T(8,128)S(1)}, f32[2,6,1792]{2,1,0:T(8,128)}, u32[]{:S(2)}) copy-start(f32[2,6,1792]{2,1,0:T(8,128)} %copy.22.refs_7_) | copy-start | bytes 258052
  13.1 106.7 %copy-start.2 = (f32[2,6,1792]{2,1,0:T(8,128)S(1)}, f32[2,6,1792]{2,1,0:T(8,128)}, u32[]{:S(2)}) copy-start(f32[2,6,1792]{2,1,0:T(8,128)} %copy.24.refs_9_) | copy-start | bytes 258052
  13.1 106.7 %copy-start.3 = (f32[2,6,1792]{2,1,0:T(8,128)S(1)}, f32[2,6,1792]{2,1,0:T(8,128)}, u32[]{:S(2)}) copy-start(f32[2,6,1792]{2,1,0:T(8,128)} %copy.25.refs_10_) | copy-start | bytes 258052
  13.1 106.7 %copy-start.4 = (f32[2,14,768]{2,1,0:T(8,128)S(1)}, f32[2,14,768]{2,1,0:T(8,128)}, u32[]{:S(2)}) copy-start(f32[2,14,768]{2,1,0:T(8,128)} %copy.23.refs_8_) | copy-start | bytes 258052
  13.1 106.7 %copy-start.5 = (f32[2,14,768]{2,1,0:T(8,128)S(1)}, f32[2,14,768]{2,1,0:T(8,128)}, u32[]{:S(2)}) copy-start(f32[2,14,768]{2,1,0:T(8,128)} %copy.26.refs_11_) | copy-start | bytes 258052
  119.8 0.9 copy-start.6
  120.7 0.9 copy-start.7
  121.6 0.9 copy-start.8

commit v2 on v0

v2 whole, which is shorter than its diff:
```python
import jax
import jax.numpy as jnp
from jax import lax
from jax.experimental import pallas as pl
from jax.experimental.pallas import tpu as pltpu
from jax.sharding import PartitionSpec as P

MESH = pl.DeviceIdType.MESH
BF, F32 = jnp.bfloat16, jnp.float32

COLS = (1792, 1792, 768)
R = (48, 48, 112)
RC = (12, 12, 28)
RP = (16, 16, 32)
H = (6, 6, 14)
AXES = ((0, 1, 2), (1, 2, 0), (2, 0, 1))
TILES = ((2, 2, 3), (2, 2, 3), (1, 1, 1))
MSGS = 25
VMEM_LIMIT = 49_500_000
ORDER = (
    1, 193, 33, 385, 225, 417, 2, 97, 257, 194, 34, 65, 481, 226, 3, 129, 418, 321, 386, 35, 195, 545, 4, 66,
    98, 258, 353, 482, 419, 227, 161, 322, 36, 130, 196, 5, 449, 546, 289, 67, 99, 354, 420, 259, 513, 483, 260, 450,
    421, 387, 100, 37, 484, 197, 162, 6, 290, 131, 323, 388, 355, 261, 514, 547, 198, 485, 451, 422, 101, 68, 228, 38,
    7, 132, 291, 389, 262, 356, 486, 8, 324, 163, 423, 452, 229, 102, 9, 548, 69, 199, 390, 263, 292, 39, 133, 357,
    515, 424, 264, 230, 164, 325, 70, 103, 200, 487, 425, 40, 10, 391, 358, 453, 549, 293, 134, 516, 41, 488, 201, 231,
    104, 265, 426, 165, 326, 71, 359, 489, 294, 550, 232, 105, 42, 72, 360, 202, 517, 427, 392, 166, 327, 135, 11, 361,
    454, 73, 551, 393, 490, 233, 295, 328, 43, 203, 518, 106, 552, 167, 136, 296, 362, 428, 455, 329, 74, 394, 168, 553,
    297, 137, 12, 44, 204, 491, 169, 107, 363, 266, 456, 330, 519, 429, 395, 234, 298, 554, 75, 457, 45, 205, 138, 108,
    520, 170, 364, 396, 331, 492, 76, 235, 13, 521, 458, 267, 299, 171, 139, 555, 430, 46, 47, 332, 109, 522, 365, 397,
    14, 15, 523, 556, 268, 459, 172, 493, 333, 431, 432, 300, 236, 398, 269, 77, 110, 140, 206, 366, 367, 524, 557, 460,
    334, 173, 494, 16, 525, 301, 461, 141, 111, 112, 433, 207, 399, 78, 270, 17, 237, 48, 558, 79, 526, 400, 174, 175,
    208, 302, 113, 142, 462, 401, 238, 368, 495, 496, 80, 559, 335, 527, 209, 369, 336, 528, 49, 143, 303, 304, 271, 272,
    463, 176, 560, 464, 529, 144, 239, 240, 337, 497, 81, 561, 273, 177, 465, 145, 305, 241,
)


def adamw(w, m, v, g):
    m = 0.9 * m + 0.1 * g
    v = 0.95 * v + 0.05 * g * g
    step = m * lax.rsqrt(v + 1e-8) + 0.1 * w
    return (w - 0.02 * step).astype(BF), m, v


class Unit:
    def __init__(self, color, chunk, way, c0, cn, uid):
        self.a, self.chunk, self.s, self.c0, self.cn, self.u = color, chunk, way, c0, cn, uid
        self.cols = pl.ds(c0, cn)


def units():
    found, uid = [], 0
    for a in range(3):
        c0 = 0
        for k, t in enumerate(TILES[a]):
            for way in (1, -1):
                found.append(Unit(a, k, way, c0, 128 * t, uid))
                c0 += 128 * t
                uid += 1
        assert c0 == COLS[a]
    return found


def comm_kernel(*refs):
    it = iter(refs)

    def take(n):
        return [next(it) for _ in range(n)]

    g, wh, mh, vh = take(3), take(3), take(3), take(3)
    out, mo, vo = take(3), take(3), take(3)
    own, part = take(3), take(3)
    psum = next(it)
    s1, r1, a1, s2, r2, a2, s3, r3 = (take(3) for _ in range(8))
    gs, gg, wx, wn, ag3, wz, wsel, m, v = (take(3) for _ in range(9))
    ag2u, tmp, osem, msem, ssem, rsem = take(6)
    all_units = units()

    me = lax.axis_index("dp")
    rep = lax.axis_index("rep")
    c = lax.rem(me, 2)
    pos = (me // 32, lax.rem(me // 8, 4), lax.rem(me // 2, 4))
    strides = (32, 8, 2)
    partner = me + 1 - 2 * c

    def near(axis, d):
        return me + (lax.rem(pos[axis] + d + 4, 4) - pos[axis]) * strides[axis]

    def send(u, i, src, dst, to):
        pltpu.make_async_remote_copy(
            src_ref=src, dst_ref=dst, send_sem=ssem.at[u.u, i], recv_sem=rsem.at[u.u, i], device_id=(rep, to), device_id_type=MESH
        ).start()

    def waiter(u, i, ref):
        return pltpu.make_async_remote_copy(
            src_ref=ref, dst_ref=ref, send_sem=ssem.at[u.u, i], recv_sem=rsem.at[u.u, i], device_id=(rep, partner), device_id_type=MESH
        )

    pending = []

    def post(u, i, src, dst, to):
        send(u, i, src, dst, to)
        pending.append((u, i, src))

    def got(u, i, ref):
        waiter(u, i, ref).wait_recv()

    def loads(u):
        return pltpu.make_async_copy(g[u.a].at[c, :, :, :, u.cols], own[u.a].at[:, :, :, u.cols], osem.at[u.u])

    def mine1(u, q, i):
        if u.a == 2:
            return psum[q, i, :, u.cols]
        at = (q, i) if u.a == 0 else (i, q)
        return own[u.a][(*at, slice(None), u.cols)].astype(F32) + part[u.a][(*at, slice(None), u.cols)].astype(F32)

    def axis(u, phase):
        return AXES[u.a][phase]

    def at(u, phase, d):
        return lax.rem(pos[axis(u, phase)] + d + 4, 4)

    S = slice(None)

    def sum1(u, i, q, came):
        @pl.loop(0, 4)
        def _(j):
            x = mine1(u, q, j)
            if came:
                x = x + r1[u.a][0, j, :, u.cols].astype(F32)
            s1[u.a][i, j, :, u.cols] = x.astype(BF)

        post(u, i, s1[u.a].at[i, :, :, u.cols], r1[u.a].at[i, :, :, u.cols], near(axis(u, 0), -u.s if i == 1 else u.s))

    def sum2(u, i, q, came):
        x = a1[u.a][q, :, u.cols]
        if came:
            x = x + r2[u.a][0, :, u.cols].astype(F32)
        s2[u.a][i, :, u.cols] = x.astype(BF)
        post(u, 3 + i, s2[u.a].at[i, :, u.cols], r2[u.a].at[i, :, u.cols], near(axis(u, 1), -u.s if i == 1 else u.s))

    def sum3(u, i, q, came):
        x = a2[u.a][q, :, u.cols]
        if came:
            x = x + r3[u.a][0, :, u.cols].astype(F32)
        s3[u.a][i, :, u.cols] = x.astype(BF)
        post(u, 6 + i, s3[u.a].at[i, :, u.cols], r3[u.a].at[i, :, u.cols], near(axis(u, 2), -u.s if i == 1 else u.s))

    def start_sum(u, phase, fn):
        fn(u, 0, at(u, phase, 2), False)
        fn(u, 1, at(u, phase, -u.s), False)

    def st0(u):
        post(u, 20, g[u.a].at[1 - c, :, :, :, u.cols], part[u.a].at[:, :, :, u.cols], partner)

    def st1(u):
        loads(u).wait()
        got(u, 20, part[u.a].at[:, :, :, u.cols])
        if u.a == 2:

            @pl.loop(0, 4)
            def _(x):
                for y in range(4):
                    t = own[2][x, y, :, u.cols].astype(F32) + part[2][x, y, :, u.cols].astype(F32)
                    for z in range(4):
                        psum[z, x, 28 * y : 28 * y + 28, u.cols] = t[28 * z : 28 * z + 28]

        start_sum(u, 0, sum1)

    def st2(u):
        got(u, 0, r1[u.a].at[0, :, :, u.cols])
        sum1(u, 2, at(u, 0, u.s), True)

    def st3(u):
        got(u, 1, r1[u.a].at[1, :, :, u.cols])
        got(u, 2, r1[u.a].at[2, :, :, u.cols])
        q = pos[axis(u, 0)]

        def total(j):
            return mine1(u, q, j) + r1[u.a][1, j, :, u.cols].astype(F32) + r1[u.a][2, j, :, u.cols].astype(F32)

        if u.a == 1:
            for j in range(4):
                t = total(j)
                for z in range(4):
                    a1[1][z, 12 * j : 12 * j + 12, u.cols] = t[12 * z : 12 * z + 12]
        else:

            @pl.loop(0, 4)
            def _(j):
                a1[u.a][j, :, u.cols] = total(j)

        start_sum(u, 1, sum2)

    def st4(u):
        got(u, 3, r2[u.a].at[0, :, u.cols])
        sum2(u, 2, at(u, 1, u.s), True)

    def st5(u):
        got(u, 4, r2[u.a].at[1, :, u.cols])
        got(u, 5, r2[u.a].at[2, :, u.cols])
        rc = RC[u.a]
        t = a1[u.a][pos[axis(u, 1)], :, u.cols] + r2[u.a][1, :, u.cols].astype(F32) + r2[u.a][2, :, u.cols].astype(F32)
        for q in range(4):
            a2[u.a][q, 0:rc, u.cols] = t[rc * q : rc * q + rc]
        start_sum(u, 2, sum3)

    def st6(u):
        got(u, 6, r3[u.a].at[0, :, u.cols])
        sum3(u, 2, at(u, 2, u.s), True)

    def st7(u):
        got(u, 7, r3[u.a].at[1, :, u.cols])
        got(u, 8, r3[u.a].at[2, :, u.cols])
        h = H[u.a]
        t = a2[u.a][pos[axis(u, 2)], :, u.cols] + r3[u.a][1, :, u.cols].astype(F32) + r3[u.a][2, :, u.cols].astype(F32)
        for q in range(2):
            gs[u.a][q, 0:h, u.cols] = t[h * q : h * q + h].astype(BF)
        post(u, 9, gs[u.a].at[1 - c, :, u.cols], gg[u.a].at[c, :, u.cols], partner)
        gg[u.a][c, 0:h, u.cols] = gs[u.a][c, 0:h, u.cols]

    def st8(u):
        got(u, 9, gg[u.a].at[1 - c, :, u.cols])
        h = H[u.a]
        for layer in range(2):
            grad = gg[u.a][layer, 0:h, u.cols].astype(F32)
            new, mn, vn = adamw(wsel[u.a][layer, 0:h, u.cols], m[u.a][:, layer, u.cols], v[u.a][:, layer, u.cols], grad)
            wn[u.a][layer, 0:h, u.cols] = new
            mo[u.a][:, layer, u.cols] = mn
            vo[u.a][:, layer, u.cols] = vn
        post(u, 10, wn[u.a].at[1 - c, :, u.cols], wx[u.a].at[c, :, u.cols], partner)

    def spread(u, base, phase, i, ref, q):
        post(u, base + i, ref(q), ref(q), near(axis(u, phase), -u.s if i == 1 else u.s))

    def start_spread(u, base, phase, ref):
        q = pos[axis(u, phase)]
        spread(u, base, phase, 0, ref, q)
        spread(u, base, phase, 1, ref, q)

    def pass_on(u, base, phase, ref):
        q = at(u, phase, -u.s)
        got(u, base, ref(q))
        spread(u, base, phase, 2, ref, q)

    def end_spread(u, base, phase, ref):
        got(u, base + 1, ref(at(u, phase, u.s)))
        got(u, base + 2, ref(at(u, phase, 2)))

    def ref3(u):
        return lambda q: ag3[u.a].at[q, :, u.cols]

    def ref2(u):
        if u.a == 0:
            return lambda q: out[0].at[c, pos[0], q, :, u.cols]
        if u.a == 1:
            return lambda q: ag2u.at[q, :, u.cols]
        return lambda q: out[2].at[c, pos[2], q, :, u.cols]

    def ref1(u, layer=c):
        if u.a == 1:
            return lambda q: out[1].at[layer, :, q, :, u.cols]
        return lambda q: out[u.a].at[layer, q, :, :, u.cols]

    def over(u, i, q):
        post(u, i, ref1(u)(q), ref1(u)(q), partner)

    def st9(u):
        got(u, 10, wx[u.a].at[1 - c, :, u.cols])
        h, rp = H[u.a], RP[u.a]
        wx[u.a][c, 0:h, u.cols] = wn[u.a][c, 0:h, u.cols]
        for q in range(2):
            tmp[h * q : h * q + h, 0 : u.cn] = wx[u.a][q, 0:h, u.cols].astype(F32)
        ag3[u.a][pos[axis(u, 2)], :, u.cols] = tmp[0:rp, 0 : u.cn].astype(BF)
        start_spread(u, 11, 2, ref3(u))

    def st10(u):
        pass_on(u, 11, 2, ref3(u))

    def st11(u):
        end_spread(u, 11, 2, ref3(u))
        rc, r = RC[u.a], R[u.a]
        for q in range(4):
            tmp[rc * q : rc * q + rc, 0 : u.cn] = ag3[u.a][q, 0:rc, u.cols].astype(F32)
        ref2(u)(pos[axis(u, 1)])[...] = tmp[0:r, 0 : u.cn].astype(BF)
        start_spread(u, 14, 1, ref2(u))

    def st12(u):
        pass_on(u, 14, 1, ref2(u))

    def st13(u):
        end_spread(u, 14, 1, ref2(u))
        if u.a == 1:
            for x in range(4):
                for z in range(4):
                    tmp[12 * z : 12 * z + 12, 0 : u.cn] = ag2u[z, 12 * x : 12 * x + 12, u.cols].astype(F32)
                out[1][c, x, pos[1], :, u.cols] = tmp[0:48, 0 : u.cn].astype(BF)
        start_spread(u, 17, 0, ref1(u))
        over(u, 21, pos[axis(u, 0)])

    def st14(u):
        pass_on(u, 17, 0, ref1(u))
        over(u, 22, at(u, 0, -u.s))

    def st15(u):
        got(u, 18, ref1(u)(at(u, 0, u.s)))
        over(u, 23, at(u, 0, u.s))

    def st16(u):
        got(u, 19, ref1(u)(at(u, 0, 2)))
        over(u, 24, at(u, 0, 2))

    def st17(u):
        theirs = ref1(u, 1 - c)
        got(u, 21, theirs(pos[axis(u, 0)]))
        got(u, 22, theirs(at(u, 0, -u.s)))
        got(u, 23, theirs(at(u, 0, u.s)))
        got(u, 24, theirs(at(u, 0, 2)))

    small = []
    for a in range(3):
        for src, dst in (
            (wh[a].at[:, pos[0], pos[1]], wz[a]),
            (mh[a], m[a]),
            (vh[a], v[a]),
        ):
            small.append(pltpu.make_async_copy(src, dst, msem.at[len(small)]))
    by_chunk = sorted(all_units, key=lambda u: (u.chunk, u.u))
    for u in by_chunk:
        loads(u).start()
    barrier = pltpu.get_barrier_semaphore()
    peers = [partner] + [near(x, d) for x in range(3) for d in (1, -1)]
    for peer in peers:
        pl.semaphore_signal(barrier, inc=1, device_id=(rep, peer), device_id_type=MESH)
    pl.semaphore_wait(barrier, len(peers))

    for u in by_chunk:
        st0(u)
    for one in small:
        one.start()
    for one in small:
        one.wait()
    rank = lax.rem(me, 8)
    for a in range(3):

        @pl.loop(0, COLS[a] // 256)
        def _(j):
            cols = pl.ds(pl.multiple_of(j * 256, 256), 256)
            h = H[a]
            for layer in range(2):
                line = wz[a][layer, :, cols].astype(F32)
                mine = line[0:h]
                for q in range(1, 8):
                    mine = jnp.where(rank == q, line[h * q : h * q + h], mine)
                wsel[a][layer, 0:h, cols] = mine

    stages = (st0, st1, st2, st3, st4, st5, st6, st7, st8, st9, st10, st11, st12, st13, st14, st15, st16, st17)
    for code in ORDER:
        stages[code % 32](all_units[code // 32])
    for u, i, src in pending:
        waiter(u, i, src).wait_send()


def finish_kernel(*refs):
    it = iter(refs)

    def take(n):
        return [next(it) for _ in range(n)]

    src, moments, out, new = take(3), take(6), take(3), take(6)
    buf, tmp, sem, bsem = take(4)
    copies = [pltpu.make_async_copy(x, y, sem.at[i]) for i, (x, y) in enumerate(zip(src[:2] + moments, out[:2] + new, strict=True))]
    for one in copies:
        one.start()

    def back(layer, x, n):
        return pltpu.make_async_copy(buf.at[n], out[2].at[layer, x], bsem.at[n])

    for layer in range(2):
        for x in range(4):
            n = 4 * layer + x

            @pl.loop(0, 3)
            def _(j):
                cols = pl.ds(pl.multiple_of(j * 256, 256), 256)
                for y in range(4):
                    for z in range(4):
                        tmp[28 * z : 28 * z + 28] = src[2][layer, z, x, 28 * y : 28 * y + 28, cols].astype(F32)
                    buf[n, y, :, cols] = tmp[...].astype(BF)

            back(layer, x, n).start()
    for layer in range(2):
        for x in range(4):
            back(layer, x, 4 * layer + x).wait()
    for one in copies:
        one.wait()


def solution(mesh):
    def step(*arrays):
        terms, weights, m, v = (arrays[i : i + 3] for i in (0, 3, 6, 9))
        whole = [(2, 4, 4, R[a], COLS[a]) for a in range(3)]
        terms = [t[0].reshape(s) for t, s in zip(terms, whole, strict=True)]
        views = [w.reshape(s) for w, s in zip(weights, whole, strict=True)]
        m, v = ([x.transpose(1, 0, 2) for x in y] for y in (m, v))
        vmem = pl.BlockSpec(memory_space=pltpu.VMEM)
        hbm = pl.BlockSpec(memory_space=pl.ANY)
        per = lambda fn, dt: [pltpu.VMEM(fn(a), dt) for a in range(3)]
        moment = lambda a: (H[a], 2, COLS[a])
        rows = lambda a: (2, 16, COLS[a])
        n = len(units())
        scratch = (
            per(lambda a: (4, 4, R[a], COLS[a]), BF) * 2
            + [pltpu.VMEM((4, 4, R[2], COLS[2]), F32)]
            + per(lambda a: (3, 4, R[a], COLS[a]), BF) * 2
            + per(lambda a: (4, R[a], COLS[a]), F32)
            + per(lambda a: (3, R[a], COLS[a]), BF) * 2
            + per(lambda a: (4, RP[a], COLS[a]), F32)
            + per(lambda a: (3, RP[a], COLS[a]), BF) * 2
            + per(rows, BF) * 4
            + per(lambda a: (4, RP[a], COLS[a]), BF)
            + per(lambda a: (2, R[a], COLS[a]), BF)
            + per(lambda a: (2, 8 if a < 2 else 16, COLS[a]), F32)
            + per(moment, F32) * 2
            + [pltpu.VMEM((4, 48, COLS[1]), BF), pltpu.VMEM((112, 128 * max(max(t) for t in TILES)), F32)]
            + [pltpu.SemaphoreType.DMA((n,)), pltpu.SemaphoreType.DMA((9,)), pltpu.SemaphoreType.DMA((n, MSGS)), pltpu.SemaphoreType.DMA((n, MSGS))]
        )
        got = pl.pallas_call(
            comm_kernel,
            out_shape=[pltpu.VMEM(s, BF) for s in whole] + per(moment, F32) * 2,
            in_specs=[hbm] * 12,
            out_specs=[vmem] * 9,
            scratch_shapes=scratch,
            compiler_params=pltpu.CompilerParams(collective_id=0, has_side_effects=True, vmem_limit_bytes=VMEM_LIMIT),
        )(*terms, *views, *m, *v)
        kept = [pltpu.with_memory_space_constraint(x, pltpu.VMEM) for x in got]
        done = pl.pallas_call(
            finish_kernel,
            out_shape=[jax.ShapeDtypeStruct(s, BF) for s in whole] + [jax.ShapeDtypeStruct(moment(a), F32) for a in range(3)] * 2,
            in_specs=[vmem] * 9,
            out_specs=[hbm] * 9,
            scratch_shapes=[
                pltpu.VMEM((8, 4, R[2], COLS[2]), BF),
                pltpu.VMEM((112, 256), F32),
                pltpu.SemaphoreType.DMA((8,)),
                pltpu.SemaphoreType.DMA((8,)),
            ],
            compiler_params=pltpu.CompilerParams(vmem_limit_bytes=20_000_000),
        )(*kept)
        return [x.reshape(w.shape) for x, w in zip(done[:3], weights, strict=True)] + [x.transpose(1, 0, 2) for x in done[3:]]

    def run(*arrays):
        return tuple(step(*arrays))

    all_of, cut = P(None, None, None), P(None, "dp", None)
    return jax.shard_map(
        run,
        mesh=mesh,
        in_specs=(P(("rep", "dp"), None, None, None),) * 3 + (all_of,) * 3 + (cut,) * 6,
        out_specs=(P("rep", None, None),) * 3 + (P("rep", "dp", None),) * 6,
        check_vma=False,
    )
```

time: 500 us -> 108 us (0.22)
  waiting for transfers between devices: 407 us -> 0 us
  Pallas kernels: 0 us -> 107 us
  local copies, waits for them, and re-layouts: 73.8 us -> 0 us
  between operations: 13.9 us -> 0.65 us
  other arithmetic: 5.04 us -> 0 us
    unnamed x5 -> x0, waiting for transfers between devices: 219 us -> none
    all_gather x3 -> x0, waiting for transfers between devices: 188 us -> none  [step(): whole = [lax.all_gather(one[0], 'dp', axis=1, tiled=True) for one in new]]
    pallas_call x0 -> x2, Pallas kernels: none -> 107 us  [the longest x1 101 us: step(): pl.pallas_call(comm_kernel, out_shape=[pltpu.VMEM(s, BF) for s in whole]...]
    unnamed x20 -> x0, local copies, waits for them, and re-layouts: 42.8 us -> none
    squeeze x1 -> x0, local copies, waits for them, and re-layouts: 28.9 us -> none  [step(): t[0]]
    convert_element_type x3 -> x0, other arithmetic: 5.04 us -> none  [adamw(): return ((w - 0.02 * step).astype(jnp.bfloat16), m, v)]
  transfers between devices with their start and end apart: 4 -> 0, of which waited for: 4 -> 0; matrix products, arithmetic and copies ran while one was open for 3% -> 0% of each run, Pallas kernels for 0% -> 0%
where the time goes in v2:
time: 108 us
  Pallas kernels  107 us (99%)
    pallas_call x1, Pallas kernels, step(): pl.pallas_call(comm_kernel, out_shape=[pltpu.VMEM(s, BF) for s in whole]...  101 us
    pallas_call x1, Pallas kernels, step(): pl.pallas_call(finish_kernel, out_shape=[jax.ShapeDtypeStruct(s, BF) for...  6.08 us

profile of v2, /device:TPU:1, one launch (start us, length us, event | category | flops | bytes accessed | tf_op | source)
XLA Modules:
  0.0 107.9 jit_solution(15175687118679865532)
XLA Ops:
  0.6 101.2 %shard_map.187 = (bf16[2,4,4,48,1792]{4,3,2,1,0:T(8,128)(2,1)S(1)}, bf16[2,4,4,48,1792]{4,3,2,1,0:T(8,128)(2,1)S(1)}, bf16[2,4,4,112,768]{4,3,2,1,0:T(8,128)(2,1...) custom-call(bf16[2,4,4,48,1792]{4,3,2,1,0:T(8,128)(2,1)} %bitcast.21, ...), custom_call_target="tpu_custom_call" | custom-call | tf_op jit(solution)/shard_map/pallas_call | solution.py:427
  101.9 6.1 %shard_map.188 = (bf16[2,4,4,48,1792]{4,3,2,1,0:T(8,128)(2,1)}, bf16[2,4,4,48,1792]{4,3,2,1,0:T(8,128)(2,1)}, bf16[2,4,4,112,768]{4,3,2,1,0:T(8,128)(2,1)}, f32[...) custom-call(bf16[2,4,4,48,1792]{4,3,2,1,0:T(8,128)(2,1)S(1)} %get-tu, ...), custom_call_target="tpu_custom_call" | custom-call | tf_op jit(solution)/shard_map/pallas_call | solution.py:436

commit v3 on v2

v3 whole, which is shorter than its diff:
```python
import jax
import jax.numpy as jnp
from jax import lax
from jax.experimental import pallas as pl
from jax.experimental.pallas import tpu as pltpu
from jax.sharding import PartitionSpec as P

MESH = pl.DeviceIdType.MESH
BF, F32 = jnp.bfloat16, jnp.float32

COLS = (1792, 1792, 768)
R = (48, 48, 112)
RC = (12, 12, 28)
RP = (16, 16, 32)
H = (6, 6, 14)
AXES = ((0, 1, 2), (1, 2, 0), (2, 0, 1))
TILES = ((2, 2, 3), (2, 2, 3), (1, 1, 1))
VMEM_LIMIT = 49_500_000
ORDER = (
    1, 97, 193, 33, 129, 98, 225, 2, 194, 34, 130, 161, 65, 226, 99, 131, 35, 195, 3, 257, 162, 66, 132, 196,
    100, 227, 258, 36, 4, 197, 67, 228, 133, 163, 37, 198, 5, 101, 259, 229, 134, 68, 164, 199, 38, 6, 102, 260,
    230, 200, 135, 69, 165, 39, 201, 7, 103, 136, 231, 261, 40, 166, 70, 137, 41, 262, 104, 202, 232, 8, 138, 167,
    71, 105, 42, 9, 233, 263, 168, 203, 72, 139, 264, 43, 169, 10, 106, 234, 73, 140, 265, 204, 170, 44, 107, 11,
    235, 266, 141, 74, 171, 45, 108, 205, 75, 267, 236, 12, 142, 46, 172, 76, 109, 206, 268, 13, 237, 173, 77, 269,
    238, 110, 47, 14, 15, 78, 174, 143, 144, 270, 111, 175, 271, 48, 207, 208, 112, 16, 79, 239, 240, 176, 272, 17,
    80, 145, 209, 241, 49, 113, 177, 273, 81,
)


def adamw(w, m, v, g):
    m = 0.9 * m + 0.1 * g
    v = 0.95 * v + 0.05 * g * g
    step = m * lax.rsqrt(v + 1e-8) + 0.1 * w
    return (w - 0.02 * step).astype(BF), m, v


class Unit:
    def __init__(self, way, c0, cn):
        self.s, self.cn, self.cols = way, cn, pl.ds(c0, cn)


class Pair:
    def __init__(self, color, chunk, uid, c0, cn):
        self.a, self.chunk, self.p, self.cn, self.cols = color, chunk, uid, cn, pl.ds(c0, cn)
        self.units = (Unit(1, c0, cn // 2), Unit(-1, c0 + cn // 2, cn // 2))


def pairs():
    found = []
    for a in range(3):
        c0 = 0
        for k, t in enumerate(TILES[a]):
            found.append(Pair(a, k, len(found), c0, 256 * t))
            c0 += 256 * t
    return found


RECV = (0, 1, 2, 3, 4, 5, 6, 7, 8, 10, 9, 3, 4, 5, 0, 1, 2, 11, 12, 13, 9, 10, 14, 15, 16)
SEND = (0, 1, 2, 0, 1, 2, 0, 1, 2, 3, 3, 0, 1, 2, 0, 1, 2, 0, 1, 2, 3, 3, 4, 5, 6)


def comm_kernel(*refs):
    it = iter(refs)

    def take(n):
        return [next(it) for _ in range(n)]

    g, wh, mh, vh = take(3), take(3), take(3), take(3)
    out, mo, vo = take(3), take(3), take(3)
    own, part = take(3), take(3)
    psum = next(it)
    s1, r1, a1, s2, r2, a2, s3, r3 = (take(3) for _ in range(8))
    gs, gg, wx, wn, ag3, wz, wsel, m, v = (take(3) for _ in range(9))
    ag2u, tmp, osem, msem, ssem, rsem = take(6)
    all_pairs = pairs()

    me = lax.axis_index("dp")
    rep = lax.axis_index("rep")
    c = lax.rem(me, 2)
    pos = (me // 32, lax.rem(me // 8, 4), lax.rem(me // 2, 4))
    strides = (32, 8, 2)
    partner = me + 1 - 2 * c

    def near(axis, d):
        return me + (lax.rem(pos[axis] + d + 4, 4) - pos[axis]) * strides[axis]

    def message(u, i, src, dst, to):
        return pltpu.make_async_remote_copy(
            src_ref=src, dst_ref=dst, send_sem=ssem.at[u.p, SEND[i]], recv_sem=rsem.at[u.p, RECV[i]], device_id=(rep, to), device_id_type=MESH
        )

    leaving = {}

    def post(u, i, sends, whole):
        key = (u.p, SEND[i])
        if key in leaving:
            leaving.pop(key)()
        for one in sends:
            message(u, i, *one).start()
        leaving[key] = lambda: message(u, i, whole, whole, partner).wait_send()

    def got(u, i, whole):
        message(u, i, whole, whole, partner).wait_recv()

    def loads(u):
        return pltpu.make_async_copy(g[u.a].at[c, :, :, :, u.cols], own[u.a].at[:, :, :, u.cols], osem.at[u.p])

    def mine1(u, cols, q, i):
        if u.a == 2:
            return psum[q, i, :, cols]
        where = (q, i) if u.a == 0 else (i, q)
        return own[u.a][(*where, slice(None), cols)].astype(F32) + part[u.a][(*where, slice(None), cols)].astype(F32)

    def mine2(u, cols, q, i):
        return a1[u.a][q, :, cols]

    def mine3(u, cols, q, i):
        return a2[u.a][q, :, cols]

    def axis(u, phase):
        return AXES[u.a][phase]

    def at(u, phase, d):
        return lax.rem(pos[axis(u, phase)] + d + 4, 4)

    mines, outs, ins = (mine1, mine2, mine3), (s1, s2, s3), (r1, r2, r3)

    def add(u, cols, phase, i, q):
        src, dst = ins[phase][u.a], outs[phase][u.a]
        if phase == 0:

            @pl.loop(0, 4)
            def _(j):
                x = mine1(u, cols, q, j)
                if i == 2:
                    x = x + src[0, j, :, cols].astype(F32)
                dst[i, j, :, cols] = x.astype(BF)

        else:
            x = mines[phase](u, cols, q, 0)
            if i == 2:
                x = x + src[0, :, cols].astype(F32)
            dst[i, :, cols] = x.astype(BF)

    def view(ref, phase, i, cols):
        return ref.at[i, :, :, cols] if phase == 0 else ref.at[i, :, cols]

    def give(u, phase, i):
        src, dst = outs[phase][u.a], ins[phase][u.a]
        if i == 0:
            add(u, u.cols, phase, 0, at(u, phase, 2))
        else:
            for t in u.units:
                add(u, t.cols, phase, i, at(u, phase, -t.s if i == 1 else t.s))
        sends = [(view(src, phase, i, t.cols), view(dst, phase, i, t.cols), near(axis(u, phase), -t.s if i == 1 else t.s)) for t in u.units]
        post(u, 3 * phase + i, sends, view(src, phase, i, u.cols))

    def take_in(u, phase, i):
        got(u, 3 * phase + i, view(ins[phase][u.a], phase, i, u.cols))

    def st0(u):
        post(u, 20, [(g[u.a].at[1 - c, :, :, :, u.cols], part[u.a].at[:, :, :, u.cols], partner)], part[u.a].at[:, :, :, u.cols])

    def st1(u):
        loads(u).wait()
        got(u, 20, part[u.a].at[:, :, :, u.cols])
        if u.a == 2:

            @pl.loop(0, 4)
            def _(x):
                for y in range(4):
                    t = own[2][x, y, :, u.cols].astype(F32) + part[2][x, y, :, u.cols].astype(F32)
                    for z in range(4):
                        psum[z, x, 28 * y : 28 * y + 28, u.cols] = t[28 * z : 28 * z + 28]

        give(u, 0, 0)
        give(u, 0, 1)

    def st2(u):
        take_in(u, 0, 0)
        give(u, 0, 2)

    def st3(u):
        take_in(u, 0, 1)
        take_in(u, 0, 2)
        q = pos[axis(u, 0)]

        def total(j):
            return mine1(u, u.cols, q, j) + r1[u.a][1, j, :, u.cols].astype(F32) + r1[u.a][2, j, :, u.cols].astype(F32)

        if u.a == 1:
            for j in range(4):
                t = total(j)
                for z in range(4):
                    a1[1][z, 12 * j : 12 * j + 12, u.cols] = t[12 * z : 12 * z + 12]
        else:

            @pl.loop(0, 4)
            def _(j):
                a1[u.a][j, :, u.cols] = total(j)

        give(u, 1, 0)
        give(u, 1, 1)

    def st4(u):
        take_in(u, 1, 0)
        give(u, 1, 2)

    def st5(u):
        take_in(u, 1, 1)
        take_in(u, 1, 2)
        rc = RC[u.a]
        t = a1[u.a][pos[axis(u, 1)], :, u.cols] + r2[u.a][1, :, u.cols].astype(F32) + r2[u.a][2, :, u.cols].astype(F32)
        for q in range(4):
            a2[u.a][q, 0:rc, u.cols] = t[rc * q : rc * q + rc]
        give(u, 2, 0)
        give(u, 2, 1)

    def st6(u):
        take_in(u, 2, 0)
        give(u, 2, 2)

    def st7(u):
        take_in(u, 2, 1)
        take_in(u, 2, 2)
        h = H[u.a]
        t = a2[u.a][pos[axis(u, 2)], :, u.cols] + r3[u.a][1, :, u.cols].astype(F32) + r3[u.a][2, :, u.cols].astype(F32)
        for q in range(2):
            gs[u.a][q, 0:h, u.cols] = t[h * q : h * q + h].astype(BF)
        post(u, 9, [(gs[u.a].at[1 - c, :, u.cols], gg[u.a].at[c, :, u.cols], partner)], gs[u.a].at[0, :, u.cols])
        gg[u.a][c, 0:h, u.cols] = gs[u.a][c, 0:h, u.cols]

    def st8(u):
        got(u, 9, gg[u.a].at[1 - c, :, u.cols])
        h = H[u.a]
        for layer in range(2):
            grad = gg[u.a][layer, 0:h, u.cols].astype(F32)
            new, mn, vn = adamw(wsel[u.a][layer, 0:h, u.cols], m[u.a][:, layer, u.cols], v[u.a][:, layer, u.cols], grad)
            wn[u.a][layer, 0:h, u.cols] = new
            mo[u.a][:, layer, u.cols] = mn
            vo[u.a][:, layer, u.cols] = vn
        post(u, 10, [(wn[u.a].at[1 - c, :, u.cols], wx[u.a].at[c, :, u.cols], partner)], wn[u.a].at[0, :, u.cols])

    def ref3(u, cols):
        return lambda q: ag3[u.a].at[q, :, cols]

    def ref2(u, cols):
        if u.a == 0:
            return lambda q: out[0].at[c, pos[0], q, :, cols]
        if u.a == 1:
            return lambda q: ag2u.at[q, :, cols]
        return lambda q: out[2].at[c, pos[2], q, :, cols]

    def ref1(u, cols, layer=c):
        if u.a == 1:
            return lambda q: out[1].at[layer, :, q, :, cols]
        return lambda q: out[u.a].at[layer, q, :, :, cols]

    refs_of = (ref1, ref2, ref3)

    def base(phase):
        return 17 - 3 * phase

    def spread(u, phase, i):
        sends = []
        for t in u.units:
            block = refs_of[phase](u, t.cols)(at(u, phase, -t.s) if i == 2 else pos[axis(u, phase)])
            sends.append((block, block, near(axis(u, phase), -t.s if i == 1 else t.s)))
        post(u, base(phase) + i, sends, refs_of[phase](u, u.cols)(pos[axis(u, phase)]))

    def start_spread(u, phase):
        spread(u, phase, 0)
        spread(u, phase, 1)

    def arrived(u, phase, i):
        got(u, base(phase) + i, refs_of[phase](u, u.cols)(at(u, phase, 2)))

    def pass_on(u, phase):
        arrived(u, phase, 0)
        spread(u, phase, 2)

    def end_spread(u, phase):
        arrived(u, phase, 1)
        arrived(u, phase, 2)

    def over(u, i, d):
        if d % 2 == 0:
            block = ref1(u, u.cols)(at(u, 0, d))
            sends = [(block, block, partner)]
        else:
            own_blocks = [ref1(u, t.cols)(at(u, 0, d * t.s)) for t in u.units]
            sends = [(x, x, partner) for x in own_blocks]
        post(u, i, sends, ref1(u, u.cols)(pos[axis(u, 0)]))

    def st9(u):
        got(u, 10, wx[u.a].at[1 - c, :, u.cols])
        h, rp = H[u.a], RP[u.a]
        wx[u.a][c, 0:h, u.cols] = wn[u.a][c, 0:h, u.cols]
        for q in range(2):
            tmp[h * q : h * q + h, 0 : u.cn] = wx[u.a][q, 0:h, u.cols].astype(F32)
        ag3[u.a][pos[axis(u, 2)], :, u.cols] = tmp[0:rp, 0 : u.cn].astype(BF)
        start_spread(u, 2)

    def st10(u):
        pass_on(u, 2)

    def st11(u):
        end_spread(u, 2)
        rc, r = RC[u.a], R[u.a]
        for q in range(4):
            tmp[rc * q : rc * q + rc, 0 : u.cn] = ag3[u.a][q, 0:rc, u.cols].astype(F32)
        ref2(u, u.cols)(pos[axis(u, 1)])[...] = tmp[0:r, 0 : u.cn].astype(BF)
        start_spread(u, 1)

    def st12(u):
        pass_on(u, 1)

    def st13(u):
        end_spread(u, 1)
        if u.a == 1:
            for x in range(4):
                for z in range(4):
                    tmp[12 * z : 12 * z + 12, 0 : u.cn] = ag2u[z, 12 * x : 12 * x + 12, u.cols].astype(F32)
                out[1][c, x, pos[1], :, u.cols] = tmp[0:48, 0 : u.cn].astype(BF)
        start_spread(u, 0)
        over(u, 21, 0)

    def st14(u):
        pass_on(u, 0)
        over(u, 22, -1)

    def st15(u):
        arrived(u, 0, 1)
        over(u, 23, 1)

    def st16(u):
        arrived(u, 0, 2)
        over(u, 24, 2)

    def st17(u):
        for i in (21, 22, 23, 24):
            got(u, i, ref1(u, u.cols, 1 - c)(pos[axis(u, 0)]))

    small = []
    for a in range(3):
        for src, dst in (
            (wh[a].at[:, pos[0], pos[1]], wz[a]),
            (mh[a], m[a]),
            (vh[a], v[a]),
        ):
            small.append(pltpu.make_async_copy(src, dst, msem.at[len(small)]))
    by_chunk = sorted(all_pairs, key=lambda u: (u.chunk, u.p))
    for u in by_chunk:
        loads(u).start()
    barrier = pltpu.get_barrier_semaphore()
    peers = [partner] + [near(x, d) for x in range(3) for d in (1, -1)]
    for peer in peers:
        pl.semaphore_signal(barrier, inc=1, device_id=(rep, peer), device_id_type=MESH)
    pl.semaphore_wait(barrier, len(peers))

    for u in by_chunk:
        st0(u)
    for one in small:
        one.start()
    for one in small:
        one.wait()
    rank = lax.rem(me, 8)
    for a in range(3):

        @pl.loop(0, COLS[a] // 256)
        def _(j):
            cols = pl.ds(pl.multiple_of(j * 256, 256), 256)
            h = H[a]
            for layer in range(2):
                line = wz[a][layer, :, cols].astype(F32)
                mine = line[0:h]
                for q in range(1, 8):
                    mine = jnp.where(rank == q, line[h * q : h * q + h], mine)
                wsel[a][layer, 0:h, cols] = mine

    stages = (st0, st1, st2, st3, st4, st5, st6, st7, st8, st9, st10, st11, st12, st13, st14, st15, st16, st17)
    for code in ORDER:
        stages[code % 32](all_pairs[code // 32])
    for wait in leaving.values():
        wait()


def finish_kernel(*refs):
    it = iter(refs)

    def take(n):
        return [next(it) for _ in range(n)]

    src, moments, out, new = take(3), take(6), take(3), take(6)
    buf, tmp, sem, bsem = take(4)
    copies = [pltpu.make_async_copy(x, y, sem.at[i]) for i, (x, y) in enumerate(zip(src[:2] + moments, out[:2] + new, strict=True))]
    for one in copies:
        one.start()

    def back(layer, x, n):
        return pltpu.make_async_copy(buf.at[n], out[2].at[layer, x], bsem.at[n])

    for layer in range(2):
        for x in range(4):
            n = 4 * layer + x

            @pl.loop(0, 3)
            def _(j):
                cols = pl.ds(pl.multiple_of(j * 256, 256), 256)
                for y in range(4):
                    for z in range(4):
                        tmp[28 * z : 28 * z + 28] = src[2][layer, z, x, 28 * y : 28 * y + 28, cols].astype(F32)
                    buf[n, y, :, cols] = tmp[...].astype(BF)

            back(layer, x, n).start()
    for layer in range(2):
        for x in range(4):
            back(layer, x, 4 * layer + x).wait()
    for one in copies:
        one.wait()


def solution(mesh):
    def step(*arrays):
        terms, weights, m, v = (arrays[i : i + 3] for i in (0, 3, 6, 9))
        whole = [(2, 4, 4, R[a], COLS[a]) for a in range(3)]
        terms = [t[0].reshape(s) for t, s in zip(terms, whole, strict=True)]
        views = [w.reshape(s) for w, s in zip(weights, whole, strict=True)]
        m, v = ([x.transpose(1, 0, 2) for x in y] for y in (m, v))
        vmem = pl.BlockSpec(memory_space=pltpu.VMEM)
        hbm = pl.BlockSpec(memory_space=pl.ANY)
        per = lambda fn, dt: [pltpu.VMEM(fn(a), dt) for a in range(3)]
        moment = lambda a: (H[a], 2, COLS[a])
        rows = lambda a: (2, 16, COLS[a])
        n = len(pairs())
        scratch = (
            per(lambda a: (4, 4, R[a], COLS[a]), BF) * 2
            + [pltpu.VMEM((4, 4, R[2], COLS[2]), F32)]
            + per(lambda a: (3, 4, R[a], COLS[a]), BF) * 2
            + per(lambda a: (4, R[a], COLS[a]), F32)
            + per(lambda a: (3, R[a], COLS[a]), BF) * 2
            + per(lambda a: (4, RP[a], COLS[a]), F32)
            + per(lambda a: (3, RP[a], COLS[a]), BF) * 2
            + per(rows, BF) * 4
            + per(lambda a: (4, RP[a], COLS[a]), BF)
            + per(lambda a: (2, R[a], COLS[a]), BF)
            + per(lambda a: (2, 8 if a < 2 else 16, COLS[a]), F32)
            + per(moment, F32) * 2
            + [pltpu.VMEM((4, 48, COLS[1]), BF), pltpu.VMEM((112, 256 * max(max(t) for t in TILES)), F32)]
            + [pltpu.SemaphoreType.DMA((n,)), pltpu.SemaphoreType.DMA((9,)), pltpu.SemaphoreType.DMA((n, 7)), pltpu.SemaphoreType.DMA((n, 17))]
        )
        got = pl.pallas_call(
            comm_kernel,
            out_shape=[pltpu.VMEM(s, BF) for s in whole] + per(moment, F32) * 2,
            in_specs=[hbm] * 12,
            out_specs=[vmem] * 9,
            scratch_shapes=scratch,
            compiler_params=pltpu.CompilerParams(collective_id=0, has_side_effects=True, vmem_limit_bytes=VMEM_LIMIT),
        )(*terms, *views, *m, *v)
        kept = [pltpu.with_memory_space_constraint(x, pltpu.VMEM) for x in got]
        done = pl.pallas_call(
            finish_kernel,
            out_shape=[jax.ShapeDtypeStruct(s, BF) for s in whole] + [jax.ShapeDtypeStruct(moment(a), F32) for a in range(3)] * 2,
            in_specs=[vmem] * 9,
            out_specs=[hbm] * 9,
            scratch_shapes=[
                pltpu.VMEM((8, 4, R[2], COLS[2]), BF),
                pltpu.VMEM((112, 256), F32),
                pltpu.SemaphoreType.DMA((8,)),
                pltpu.SemaphoreType.DMA((8,)),
            ],
            compiler_params=pltpu.CompilerParams(vmem_limit_bytes=20_000_000),
        )(*kept)
        return [x.reshape(w.shape) for x, w in zip(done[:3], weights, strict=True)] + [x.transpose(1, 0, 2) for x in done[3:]]

    def run(*arrays):
        return tuple(step(*arrays))

    all_of, cut = P(None, None, None), P(None, "dp", None)
    return jax.shard_map(
        run,
        mesh=mesh,
        in_specs=(P(("rep", "dp"), None, None, None),) * 3 + (all_of,) * 3 + (cut,) * 6,
        out_specs=(P("rep", None, None),) * 3 + (P("rep", "dp", None),) * 6,
        check_vma=False,
    )
```

time: 108 us -> 100 us (0.926)
  Pallas kernels: 107 us -> 99.7 us
    pallas_call x1, Pallas kernels: 101 us -> 93.6 us  [step(): pl.pallas_call(comm_kernel, out_shape=[pltpu.VMEM(s, BF) for s in whole]...]
where the time goes in v3:
time: 100 us
  Pallas kernels  99.7 us (100%)
    pallas_call x1, Pallas kernels, step(): pl.pallas_call(comm_kernel, out_shape=[pltpu.VMEM(s, BF) for s in whole]...  93.6 us
    pallas_call x1, Pallas kernels, step(): pl.pallas_call(finish_kernel, out_shape=[jax.ShapeDtypeStruct(s, BF) for...  6.08 us

profile of v3, /device:TPU:1, one launch (start us, length us, event | category | flops | bytes accessed | tf_op | source)
XLA Modules:
  0.0 100.3 jit_solution(4431695977771194985)
XLA Ops:
  0.6 93.6 %shard_map.187 = (bf16[2,4,4,48,1792]{4,3,2,1,0:T(8,128)(2,1)S(1)}, bf16[2,4,4,48,1792]{4,3,2,1,0:T(8,128)(2,1)S(1)}, bf16[2,4,4,112,768]{4,3,2,1,0:T(8,128)(2,1...) custom-call(bf16[2,4,4,48,1792]{4,3,2,1,0:T(8,128)(2,1)} %bitcast.21, ...), custom_call_target="tpu_custom_call" | custom-call | tf_op jit(solution)/shard_map/pallas_call | solution.py:452
  94.3 6.1 %shard_map.188 = (bf16[2,4,4,48,1792]{4,3,2,1,0:T(8,128)(2,1)}, bf16[2,4,4,48,1792]{4,3,2,1,0:T(8,128)(2,1)}, bf16[2,4,4,112,768]{4,3,2,1,0:T(8,128)(2,1)}, f32[...) custom-call(bf16[2,4,4,48,1792]{4,3,2,1,0:T(8,128)(2,1)S(1)} %get-tu, ...), custom_call_target="tpu_custom_call" | custom-call | tf_op jit(solution)/shard_map/pallas_call | solution.py:461

commit v4 on v3

--- a/solution.py
+++ b/solution.py
@@ -14,24 +14,22 @@
 RP = (16, 16, 32)
 H = (6, 6, 14)
 AXES = ((0, 1, 2), (1, 2, 0), (2, 0, 1))
-TILES = ((2, 2, 3), (2, 2, 3), (1, 1, 1))
+TILES = ((1, 2, 2, 2), (1, 2, 2, 2), (1, 1, 1))
 VMEM_LIMIT = 49_500_000
 ORDER = (
-    1, 97, 193, 33, 129, 98, 225, 2, 194, 34, 130, 161, 65, 226, 99, 131, 35, 195, 3, 257, 162, 66, 132, 196,
-    100, 227, 258, 36, 4, 197, 67, 228, 133, 163, 37, 198, 5, 101, 259, 229, 134, 68, 164, 199, 38, 6, 102, 260,
-    230, 200, 135, 69, 165, 39, 201, 7, 103, 136, 231, 261, 40, 166, 70, 137, 41, 262, 104, 202, 232, 8, 138, 167,
-    71, 105, 42, 9, 233, 263, 168, 203, 72, 139, 264, 43, 169, 10, 106, 234, 73, 140, 265, 204, 170, 44, 107, 11,
-    235, 266, 141, 74, 171, 45, 108, 205, 75, 267, 236, 12, 142, 46, 172, 76, 109, 206, 268, 13, 237, 173, 77, 269,
-    238, 110, 47, 14, 15, 78, 174, 143, 144, 270, 111, 175, 271, 48, 207, 208, 112, 16, 79, 239, 240, 176, 272, 17,
-    80, 145, 209, 241, 49, 113, 177, 273, 81,
+    "aaeeiibbfjeafbigdfejjcbhaieddkbgfgkihecacjbfikh",
+    "gedfbacijkhedgfcbakjhidgecbfkiahjedbeefcgaiikih",
+    "jeebbdcfgahjdikacffgbhjjjfkabaacccghikadeiegjfe",
+    "bbijjkahhcddhhkgggkdgcijffkachcdhfkdkdghjbckdg",
 )
+FIRST, PREPARE = 2, 18
 
 
 def adamw(w, m, v, g):
     m = 0.9 * m + 0.1 * g
     v = 0.95 * v + 0.05 * g * g
     step = m * lax.rsqrt(v + 1e-8) + 0.1 * w
-    return (w - 0.02 * step).astype(BF), m, v
+    return w - 0.02 * step, m, v
 
 
 class Unit:
@@ -55,8 +53,8 @@
     return found
 
 
-RECV = (0, 1, 2, 3, 4, 5, 6, 7, 8, 10, 9, 3, 4, 5, 0, 1, 2, 11, 12, 13, 9, 10, 14, 15, 16)
-SEND = (0, 1, 2, 0, 1, 2, 0, 1, 2, 3, 3, 0, 1, 2, 0, 1, 2, 0, 1, 2, 3, 3, 4, 5, 6)
+RECV = (0, 1, 2, 3, 4, 5, 6, 3, 0, 1, 2, 7, 8, 9, 10, 11, 12)
+SEND = (0, 1, 2, 0, 1, 2, 3, 3, 0, 1, 2, 0, 1, 2, 4, 4, 5)
 
 
 def comm_kernel(*refs):
@@ -70,8 +68,8 @@
     own, part = take(3), take(3)
     psum = next(it)
     s1, r1, a1, s2, r2, a2, s3, r3 = (take(3) for _ in range(8))
-    gs, gg, wx, wn, ag3, wz, wsel, m, v = (take(3) for _ in range(9))
-    ag2u, tmp, osem, msem, ssem, rsem = take(6)
+    ag3, wz, wsel, msel, vsel, ms, vs, m, v, pm, pv = (take(3) for _ in range(11))
+    ag2u, tmp, osem, msem, psem, qsem, ssem, rsem = take(8)
     all_pairs = pairs()
 
     me = lax.axis_index("dp")
@@ -93,7 +91,7 @@
 
     def post(u, i, sends, whole):
         key = (u.p, SEND[i])
-        if key in leaving:
+        if key in leaving and i != 16:
             leaving.pop(key)()
         for one in sends:
             message(u, i, *one).start()
@@ -155,15 +153,22 @@
         sends = [(view(src, phase, i, t.cols), view(dst, phase, i, t.cols), near(axis(u, phase), -t.s if i == 1 else t.s)) for t in u.units]
         post(u, 3 * phase + i, sends, view(src, phase, i, u.cols))
 
+    def give_all(u):
+        sends = []
+        for n, d in enumerate((2, 1, -1)):
+            s3[u.a][n, :, u.cols] = a2[u.a][at(u, 2, d), :, u.cols].astype(BF)
+            sends.append((s3[u.a].at[n, :, u.cols], r3[u.a].at[n, :, u.cols], near(axis(u, 2), d)))
+        post(u, 6, sends, s3[u.a].at[:, :, u.cols])
+
     def take_in(u, phase, i):
         got(u, 3 * phase + i, view(ins[phase][u.a], phase, i, u.cols))
 
+    def swap(u):
+        post(u, 14, [(g[u.a].at[1 - c, :, :, :, u.cols], part[u.a].at[:, :, :, u.cols], partner)], part[u.a].at[:, :, :, u.cols])
+
     def st0(u):
-        post(u, 20, [(g[u.a].at[1 - c, :, :, :, u.cols], part[u.a].at[:, :, :, u.cols], partner)], part[u.a].at[:, :, :, u.cols])
-
-    def st1(u):
         loads(u).wait()
-        got(u, 20, part[u.a].at[:, :, :, u.cols])
+        got(u, 14, part[u.a].at[:, :, :, u.cols])
         if u.a == 2:
 
             @pl.loop(0, 4)
@@ -174,6 +179,8 @@
                         psum[z, x, 28 * y : 28 * y + 28, u.cols] = t[28 * z : 28 * z + 28]
 
         give(u, 0, 0)
+
+    def st1(u):
         give(u, 0, 1)
 
     def st2(u):
@@ -213,36 +220,27 @@
         t = a1[u.a][pos[axis(u, 1)], :, u.cols] + r2[u.a][1, :, u.cols].astype(F32) + r2[u.a][2, :, u.cols].astype(F32)
         for q in range(4):
             a2[u.a][q, 0:rc, u.cols] = t[rc * q : rc * q + rc]
-        give(u, 2, 0)
-        give(u, 2, 1)
+        give_all(u)
 
     def st6(u):
-        take_in(u, 2, 0)
-        give(u, 2, 2)
-
-    def st7(u):
-        take_in(u, 2, 1)
-        take_in(u, 2, 2)
-        h = H[u.a]
-        t = a2[u.a][pos[axis(u, 2)], :, u.cols] + r3[u.a][1, :, u.cols].astype(F32) + r3[u.a][2, :, u.cols].astype(F32)
+        got(u, 6, r3[u.a].at[:, :, u.cols])
+        h, rp = H[u.a], RP[u.a]
+        t = a2[u.a][pos[axis(u, 2)], :, u.cols]
+        for n in range(3):
+            t = t + r3[u.a][n, :, u.cols].astype(F32)
         for q in range(2):
-            gs[u.a][q, 0:h, u.cols] = t[h * q : h * q + h].astype(BF)
-        post(u, 9, [(gs[u.a].at[1 - c, :, u.cols], gg[u.a].at[c, :, u.cols], partner)], gs[u.a].at[0, :, u.cols])
-        gg[u.a][c, 0:h, u.cols] = gs[u.a][c, 0:h, u.cols]
-
-    def st8(u):
-        got(u, 9, gg[u.a].at[1 - c, :, u.cols])
-        h = H[u.a]
-        for layer in range(2):
-            grad = gg[u.a][layer, 0:h, u.cols].astype(F32)
-            new, mn, vn = adamw(wsel[u.a][layer, 0:h, u.cols], m[u.a][:, layer, u.cols], v[u.a][:, layer, u.cols], grad)
-            wn[u.a][layer, 0:h, u.cols] = new
-            mo[u.a][:, layer, u.cols] = mn
-            vo[u.a][:, layer, u.cols] = vn
-        post(u, 10, [(wn[u.a].at[1 - c, :, u.cols], wx[u.a].at[c, :, u.cols], partner)], wn[u.a].at[0, :, u.cols])
-
-    def ref3(u, cols):
-        return lambda q: ag3[u.a].at[q, :, cols]
+            grad = t[h * q : h * q + h].astype(BF).astype(F32)
+            new, mn, vn = adamw(wsel[u.a][q, 0:h, u.cols], msel[u.a][q, 0:h, u.cols], vsel[u.a][q, 0:h, u.cols], grad)
+            tmp[h * q : h * q + h, 0 : u.cn] = new
+            ms[u.a][q, 0:h, u.cols] = mn
+            vs[u.a][q, 0:h, u.cols] = vn
+        ag3[u.a][pos[axis(u, 2)], :, u.cols] = tmp[0:rp, 0 : u.cn].astype(BF)
+        block = ag3[u.a].at[pos[axis(u, 2)], :, u.cols]
+        post(u, 7, [(block, block, near(axis(u, 2), d)) for d in (2, 1, -1)], ag3[u.a].at[0:3, :, u.cols])
+        pairs_of = [(x[u.a].at[1 - c, :, u.cols], y[u.a].at[c, :, u.cols], partner) for x, y in ((ms, mo), (vs, vo))]
+        post(u, 15, pairs_of, ms[u.a].at[:, :, u.cols])
+        for x, y in ((ms, mo), (vs, vo)):
+            y[u.a][c, 0:h, u.cols] = x[u.a][c, 0:h, u.cols]
 
     def ref2(u, cols):
         if u.a == 0:
@@ -256,10 +254,10 @@
             return lambda q: out[1].at[layer, :, q, :, cols]
         return lambda q: out[u.a].at[layer, q, :, :, cols]
 
-    refs_of = (ref1, ref2, ref3)
+    refs_of = (ref1, ref2)
 
     def base(phase):
-        return 17 - 3 * phase
+        return 11 - 3 * phase
 
     def spread(u, phase, i):
         sends = []
@@ -268,119 +266,127 @@
             sends.append((block, block, near(axis(u, phase), -t.s if i == 1 else t.s)))
         post(u, base(phase) + i, sends, refs_of[phase](u, u.cols)(pos[axis(u, phase)]))
 
-    def start_spread(u, phase):
-        spread(u, phase, 0)
-        spread(u, phase, 1)
-
     def arrived(u, phase, i):
         got(u, base(phase) + i, refs_of[phase](u, u.cols)(at(u, phase, 2)))
 
-    def pass_on(u, phase):
-        arrived(u, phase, 0)
-        spread(u, phase, 2)
-
-    def end_spread(u, phase):
-        arrived(u, phase, 1)
-        arrived(u, phase, 2)
-
-    def over(u, i, d):
+    def over(u, d):
         if d % 2 == 0:
             block = ref1(u, u.cols)(at(u, 0, d))
             sends = [(block, block, partner)]
         else:
-            own_blocks = [ref1(u, t.cols)(at(u, 0, d * t.s)) for t in u.units]
-            sends = [(x, x, partner) for x in own_blocks]
-        post(u, i, sends, ref1(u, u.cols)(pos[axis(u, 0)]))
-
-    def st9(u):
-        got(u, 10, wx[u.a].at[1 - c, :, u.cols])
-        h, rp = H[u.a], RP[u.a]
-        wx[u.a][c, 0:h, u.cols] = wn[u.a][c, 0:h, u.cols]
-        for q in range(2):
-            tmp[h * q : h * q + h, 0 : u.cn] = wx[u.a][q, 0:h, u.cols].astype(F32)
-        ag3[u.a][pos[axis(u, 2)], :, u.cols] = tmp[0:rp, 0 : u.cn].astype(BF)
-        start_spread(u, 2)
-
-    def st10(u):
-        pass_on(u, 2)
-
-    def st11(u):
-        end_spread(u, 2)
+            blocks = [ref1(u, t.cols)(at(u, 0, d * t.s)) for t in u.units]
+            sends = [(x, x, partner) for x in blocks]
+        post(u, 16, sends, out[u.a].at[c, :, :, :, u.cols])
+
+    def st7(u):
+        got(u, 7, ag3[u.a].at[0:3, :, u.cols])
         rc, r = RC[u.a], R[u.a]
         for q in range(4):
             tmp[rc * q : rc * q + rc, 0 : u.cn] = ag3[u.a][q, 0:rc, u.cols].astype(F32)
         ref2(u, u.cols)(pos[axis(u, 1)])[...] = tmp[0:r, 0 : u.cn].astype(BF)
-        start_spread(u, 1)
-
-    def st12(u):
-        pass_on(u, 1)
-
-    def st13(u):
-        end_spread(u, 1)
+        spread(u, 1, 0)
+        spread(u, 1, 1)
+
+    def st8(u):
+        arrived(u, 1, 0)
+        spread(u, 1, 2)
+
+    def st9(u):
+        arrived(u, 1, 1)
+        arrived(u, 1, 2)
         if u.a == 1:
             for x in range(4):
                 for z in range(4):
                     tmp[12 * z : 12 * z + 12, 0 : u.cn] = ag2u[z, 12 * x : 12 * x + 12, u.cols].astype(F32)
                 out[1][c, x, pos[1], :, u.cols] = tmp[0:48, 0 : u.cn].astype(BF)
-        start_spread(u, 0)
-        over(u, 21, 0)
+        spread(u, 0, 0)
+
+    def st10(u):
+        spread(u, 0, 1)
+
+    def st11(u):
+        over(u, 0)
+
+    def st12(u):
+        arrived(u, 0, 0)
+        spread(u, 0, 2)
+
+    def st13(u):
+        over(u, -1)
 
     def st14(u):
-        pass_on(u, 0)
-        over(u, 22, -1)
+        arrived(u, 0, 1)
+        over(u, 1)
 
     def st15(u):
-        arrived(u, 0, 1)
-        over(u, 23, 1)
+        arrived(u, 0, 2)
+        over(u, 2)
 
     def st16(u):
-        arrived(u, 0, 2)
-        over(u, 24, 2)
-
-    def st17(u):
-        for i in (21, 22, 23, 24):
-            got(u, i, ref1(u, u.cols, 1 - c)(pos[axis(u, 0)]))
-
-    small = []
+        got(u, 15, mo[u.a].at[:, :, u.cols])
+        got(u, 16, out[u.a].at[1 - c, :, :, :, u.cols])
+
+    small, swaps = [], []
     for a in range(3):
-        for src, dst in (
-            (wh[a].at[:, pos[0], pos[1]], wz[a]),
-            (mh[a], m[a]),
-            (vh[a], v[a]),
-        ):
-            small.append(pltpu.make_async_copy(src, dst, msem.at[len(small)]))
-    by_chunk = sorted(all_pairs, key=lambda u: (u.chunk, u.p))
+        small.append((wh[a].at[c, pos[0], pos[1]], wz[a]))
+        small.append((mh[a], m[a]))
+        small.append((vh[a], v[a]))
+        swaps.append((mh[a], pm[a]))
+        swaps.append((vh[a], pv[a]))
+    small = [pltpu.make_async_copy(src, dst, msem.at[n]) for n, (src, dst) in enumerate(small)]
+    swaps = [
+        pltpu.make_async_remote_copy(
+            src_ref=src, dst_ref=dst, send_sem=psem.at[n], recv_sem=qsem.at[n], device_id=(rep, partner), device_id_type=MESH
+        )
+        for n, (src, dst) in enumerate(swaps)
+    ]
+
+    def prepare():
+        for one in small:
+            one.wait()
+        for one in swaps:
+            one.wait()
+        for a in range(3):
+            h = H[a]
+            for src, theirs, dst in ((m, pm, msel), (v, pv, vsel)):
+                dst[a][c, 0:h] = jnp.where(c == 0, src[a][:, 0], src[a][:, 1])
+                dst[a][1 - c, 0:h] = jnp.where(c == 0, theirs[a][:, 0], theirs[a][:, 1])
+
+            @pl.loop(0, COLS[a] // 256)
+            def _(j):
+                cols = pl.ds(pl.multiple_of(j * 256, 256), 256)
+                line = wz[a][:, cols].astype(F32)
+                for q in range(2):
+                    rows = line[h * q : h * q + h]
+                    for z in range(1, 4):
+                        rows = jnp.where(pos[2] == z, line[h * (2 * z + q) : h * (2 * z + q) + h], rows)
+                    wsel[a][q, 0:h, cols] = rows
+
+    by_chunk = sorted(all_pairs, key=lambda u: ((u.chunk + 1) / len(TILES[u.a]), u.p))
     for u in by_chunk:
         loads(u).start()
     barrier = pltpu.get_barrier_semaphore()
-    peers = [partner] + [near(x, d) for x in range(3) for d in (1, -1)]
+    peers = [partner] + [near(x, d) for x in range(3) for d in (1, -1, 2)]
     for peer in peers:
         pl.semaphore_signal(barrier, inc=1, device_id=(rep, peer), device_id_type=MESH)
     pl.semaphore_wait(barrier, len(peers))
 
-    for u in by_chunk:
-        st0(u)
-    for one in small:
-        one.start()
-    for one in small:
-        one.wait()
-    rank = lax.rem(me, 8)
-    for a in range(3):
-
-        @pl.loop(0, COLS[a] // 256)
-        def _(j):
-            cols = pl.ds(pl.multiple_of(j * 256, 256), 256)
-            h = H[a]
-            for layer in range(2):
-                line = wz[a][layer, :, cols].astype(F32)
-                mine = line[0:h]
-                for q in range(1, 8):
-                    mine = jnp.where(rank == q, line[h * q : h * q + h], mine)
-                wsel[a][layer, 0:h, cols] = mine
-
-    stages = (st0, st1, st2, st3, st4, st5, st6, st7, st8, st9, st10, st11, st12, st13, st14, st15, st16, st17)
-    for code in ORDER:
-        stages[code % 32](all_pairs[code // 32])
+    for n, u in enumerate(by_chunk):
+        swap(u)
+        if n == FIRST:
+            for one in swaps:
+                one.start()
+            for one in small:
+                one.start()
+
+    stages = (st0, st1, st2, st3, st4, st5, st6, st7, st8, st9, st10, st11, st12, st13, st14, st15, st16)
+    done = [0] * len(all_pairs)
+    for n, letter in enumerate("".join(ORDER)):
+        p = "abcdefghijklmnop".index(letter)
+        stages[done[p]](all_pairs[p])
+        done[p] += 1
+        if n == PREPARE:
+            prepare()
     for wait in leaving.values():
         wait()
 
@@ -393,9 +399,14 @@
 
     src, moments, out, new = take(3), take(6), take(3), take(6)
     buf, tmp, sem, bsem = take(4)
-    copies = [pltpu.make_async_copy(x, y, sem.at[i]) for i, (x, y) in enumerate(zip(src[:2] + moments, out[:2] + new, strict=True))]
-    for one in copies:
+    turned = take(6)
+    copies = [pltpu.make_async_copy(x, y, sem.at[i]) for i, (x, y) in enumerate(zip(src[:2] + turned, out[:2] + new, strict=True))]
+    for one in copies[:2]:
         one.start()
+    for n in range(6):
+        for layer in range(2):
+            turned[n][:, layer] = moments[n][layer, 0 : H[n % 3]]
+        copies[2 + n].start()
 
     def back(layer, x, n):
         return pltpu.make_async_copy(buf.at[n], out[2].at[layer, x], bsem.at[n])
@@ -431,7 +442,7 @@
         hbm = pl.BlockSpec(memory_space=pl.ANY)
         per = lambda fn, dt: [pltpu.VMEM(fn(a), dt) for a in range(3)]
         moment = lambda a: (H[a], 2, COLS[a])
-        rows = lambda a: (2, 16, COLS[a])
+        rows = lambda a: (2, 8 if a < 2 else 16, COLS[a])
         n = len(pairs())
         scratch = (
             per(lambda a: (4, 4, R[a], COLS[a]), BF) * 2
@@ -441,17 +452,17 @@
             + per(lambda a: (3, R[a], COLS[a]), BF) * 2
             + per(lambda a: (4, RP[a], COLS[a]), F32)
             + per(lambda a: (3, RP[a], COLS[a]), BF) * 2
-            + per(rows, BF) * 4
             + per(lambda a: (4, RP[a], COLS[a]), BF)
-            + per(lambda a: (2, R[a], COLS[a]), BF)
-            + per(lambda a: (2, 8 if a < 2 else 16, COLS[a]), F32)
-            + per(moment, F32) * 2
+            + per(lambda a: (R[a], COLS[a]), BF)
+            + per(rows, F32) * 5
+            + per(moment, F32) * 4
             + [pltpu.VMEM((4, 48, COLS[1]), BF), pltpu.VMEM((112, 256 * max(max(t) for t in TILES)), F32)]
-            + [pltpu.SemaphoreType.DMA((n,)), pltpu.SemaphoreType.DMA((9,)), pltpu.SemaphoreType.DMA((n, 7)), pltpu.SemaphoreType.DMA((n, 17))]
+            + [pltpu.SemaphoreType.DMA((k,)) for k in (n, 9, 6, 6)]
+            + [pltpu.SemaphoreType.DMA((n, max(SEND) + 1)), pltpu.SemaphoreType.DMA((n, max(RECV) + 1))]
         )
         got = pl.pallas_call(
             comm_kernel,
-            out_shape=[pltpu.VMEM(s, BF) for s in whole] + per(moment, F32) * 2,
+            out_shape=[pltpu.VMEM(s, BF) for s in whole] + per(rows, F32) * 2,
             in_specs=[hbm] * 12,
             out_specs=[vmem] * 9,
             scratch_shapes=scratch,
@@ -468,7 +479,8 @@
                 pltpu.VMEM((112, 256), F32),
                 pltpu.SemaphoreType.DMA((8,)),
                 pltpu.SemaphoreType.DMA((8,)),
-            ],
+            ]
+            + per(moment, F32) * 2,
             compiler_params=pltpu.CompilerParams(vmem_limit_bytes=20_000_000),
         )(*kept)
         return [x.reshape(w.shape) for x, w in zip(done[:3], weights, strict=True)] + [x.transpose(1, 0, 2) for x in done[3:]]

time: 100 us -> 88.9 us (0.89)
  Pallas kernels: 99.7 us -> 88.1 us
    pallas_call x1, Pallas kernels: 93.6 us -> 82.1 us  [step(): pl.pallas_call(comm_kernel, out_shape=[pltpu.VMEM(s, BF) for s in whole]...]
where the time goes in v4:
time: 88.9 us; the launch traced here: 88.8 us
  Pallas kernels  88.1 us (99%)
    pallas_call x1, Pallas kernels, step(): pl.pallas_call(comm_kernel, out_shape=[pltpu.VMEM(s, BF) for s in whole]...  82.1 us
    pallas_call x1, Pallas kernels, step(): pl.pallas_call(finish_kernel, out_shape=[jax.ShapeDtypeStruct(s, BF) for...  6.08 us

profile of v4, /device:TPU:1, one launch (start us, length us, event | category | flops | bytes accessed | tf_op | source)
XLA Modules:
  0.0 88.8 jit_solution(11221374271449086786)
XLA Ops:
  0.6 82.1 %shard_map.187 = (bf16[2,4,4,48,1792]{4,3,2,1,0:T(8,128)(2,1)S(1)}, bf16[2,4,4,48,1792]{4,3,2,1,0:T(8,128)(2,1)S(1)}, bf16[2,4,4,112,768]{4,3,2,1,0:T(8,128)(2,1...) custom-call(bf16[2,4,4,48,1792]{4,3,2,1,0:T(8,128)(2,1)} %bitcast.21, ...), custom_call_target="tpu_custom_call" | custom-call | tf_op jit(solution)/shard_map/pallas_call | solution.py:463
  82.7 6.1 %shard_map.188 = (bf16[2,4,4,48,1792]{4,3,2,1,0:T(8,128)(2,1)}, bf16[2,4,4,48,1792]{4,3,2,1,0:T(8,128)(2,1)}, bf16[2,4,4,112,768]{4,3,2,1,0:T(8,128)(2,1)}, f32[...) custom-call(bf16[2,4,4,48,1792]{4,3,2,1,0:T(8,128)(2,1)S(1)} %get-tu, ...), custom_call_target="tpu_custom_call" | custom-call | tf_op jit(solution)/shard_map/pallas_call | solution.py:472

commit v5 on v4

--- a/solution.py
+++ b/solution.py
@@ -22,7 +22,7 @@
     "jeebbdcfgahjdikacffgbhjjjfkabaacccghikadeiegjfe",
     "bbijjkahhcddhhkgggkdgcijffkachcdhfkdkdghjbckdg",
 )
-FIRST, PREPARE = 2, 18
+FIRST, PREPARE = 5, 30
 
 
 def adamw(w, m, v, g):
@@ -53,8 +53,9 @@
     return found
 
 
-RECV = (0, 1, 2, 3, 4, 5, 6, 3, 0, 1, 2, 7, 8, 9, 10, 11, 12)
-SEND = (0, 1, 2, 0, 1, 2, 3, 3, 0, 1, 2, 0, 1, 2, 4, 4, 5)
+RECV = (0, 1, 1, 2, 3, 3, 4, 2, 0, 1, 1, 5, 6, 7, 8, 9, 10)
+SEND = (0, 0, 0, 1, 1, 1, 2, 2, 0, 0, 0, 1, 1, 1, 3, 3, 4)
+SAME = [range(i - i % 3, i - i % 3 + 3) if i < 6 else range(i - (i + 1) % 3, i - (i + 1) % 3 + 3) if 8 <= i < 14 else (i,) for i in range(17)]
 
 
 def comm_kernel(*refs):
@@ -79,8 +80,11 @@
     strides = (32, 8, 2)
     partner = me + 1 - 2 * c
 
+    ahead = [[lax.rem(pos[x] + d, 4) for d in range(4)] for x in range(3)]
+    nearby = [[me + (ahead[x][d] - pos[x]) * strides[x] for d in range(4)] for x in range(3)]
+
     def near(axis, d):
-        return me + (lax.rem(pos[axis] + d + 4, 4) - pos[axis]) * strides[axis]
+        return nearby[axis][d % 4]
 
     def message(u, i, src, dst, to):
         return pltpu.make_async_remote_copy(
@@ -91,11 +95,11 @@
 
     def post(u, i, sends, whole):
         key = (u.p, SEND[i])
-        if key in leaving and i != 16:
-            leaving.pop(key)()
+        if key in leaving and leaving[key][0] not in SAME[i]:
+            leaving.pop(key)[1]()
         for one in sends:
             message(u, i, *one).start()
-        leaving[key] = lambda: message(u, i, whole, whole, partner).wait_send()
+        leaving[key] = i, lambda: message(u, i, whole, whole, partner).wait_send()
 
     def got(u, i, whole):
         message(u, i, whole, whole, partner).wait_recv()
@@ -119,7 +123,7 @@
         return AXES[u.a][phase]
 
     def at(u, phase, d):
-        return lax.rem(pos[axis(u, phase)] + d + 4, 4)
+        return ahead[axis(u, phase)][d % 4]
 
     mines, outs, ins = (mine1, mine2, mine3), (s1, s2, s3), (r1, r2, r3)
 
@@ -142,6 +146,7 @@
 
     def view(ref, phase, i, cols):
         return ref.at[i, :, :, cols] if phase == 0 else ref.at[i, :, cols]
+
 
     def give(u, phase, i):
         src, dst = outs[phase][u.a], ins[phase][u.a]
@@ -151,7 +156,7 @@
             for t in u.units:
                 add(u, t.cols, phase, i, at(u, phase, -t.s if i == 1 else t.s))
         sends = [(view(src, phase, i, t.cols), view(dst, phase, i, t.cols), near(axis(u, phase), -t.s if i == 1 else t.s)) for t in u.units]
-        post(u, 3 * phase + i, sends, view(src, phase, i, u.cols))
+        post(u, 3 * phase + i, sends, view(src, phase, slice(None), u.cols))
 
     def give_all(u):
         sends = []
@@ -188,8 +193,7 @@
         give(u, 0, 2)
 
     def st3(u):
-        take_in(u, 0, 1)
-        take_in(u, 0, 2)
+        got(u, 1, view(r1[u.a], 0, slice(1, 3), u.cols))
         q = pos[axis(u, 0)]
 
         def total(j):
@@ -214,8 +218,7 @@
         give(u, 1, 2)
 
     def st5(u):
-        take_in(u, 1, 1)
-        take_in(u, 1, 2)
+        got(u, 4, view(r2[u.a], 1, slice(1, 3), u.cols))
         rc = RC[u.a]
         t = a1[u.a][pos[axis(u, 1)], :, u.cols] + r2[u.a][1, :, u.cols].astype(F32) + r2[u.a][2, :, u.cols].astype(F32)
         for q in range(4):
@@ -264,10 +267,13 @@
         for t in u.units:
             block = refs_of[phase](u, t.cols)(at(u, phase, -t.s) if i == 2 else pos[axis(u, phase)])
             sends.append((block, block, near(axis(u, phase), -t.s if i == 1 else t.s)))
-        post(u, base(phase) + i, sends, refs_of[phase](u, u.cols)(pos[axis(u, phase)]))
+        post(u, base(phase) + i, sends, thrice(u, phase))
 
     def arrived(u, phase, i):
         got(u, base(phase) + i, refs_of[phase](u, u.cols)(at(u, phase, 2)))
+
+    def thrice(u, phase):
+        return out[u.a].at[c, 0:3, :, :, u.cols] if phase == 0 else out[u.a].at[c, 0, 0:3, :, u.cols]
 
     def over(u, d):
         if d % 2 == 0:
@@ -292,8 +298,7 @@
         spread(u, 1, 2)
 
     def st9(u):
-        arrived(u, 1, 1)
-        arrived(u, 1, 2)
+        got(u, 9, out[u.a].at[c, 0, 0:2, :, u.cols])
         if u.a == 1:
             for x in range(4):
                 for z in range(4):
@@ -387,7 +392,7 @@
         done[p] += 1
         if n == PREPARE:
             prepare()
-    for wait in leaving.values():
+    for _, wait in leaving.values():
         wait()
 
 

time: 88.9 us -> 88.3 us (level)
  no operation moved by 1% of the time
where the time goes in v5:
time: 88.3 us; the launch traced here: 88.2 us
  Pallas kernels  87.6 us (99%)
    pallas_call x1, Pallas kernels, step(): pl.pallas_call(comm_kernel, out_shape=[pltpu.VMEM(s, BF) for s in whole]...  81.5 us
    pallas_call x1, Pallas kernels, step(): pl.pallas_call(finish_kernel, out_shape=[jax.ShapeDtypeStruct(s, BF) for...  6.08 us

profile of v5, /device:TPU:1, one launch (start us, length us, event | category | flops | bytes accessed | tf_op | source)
XLA Modules:
  0.0 88.2 jit_solution(4973920950011531422)
XLA Ops:
  0.6 81.5 %shard_map.187 = (bf16[2,4,4,48,1792]{4,3,2,1,0:T(8,128)(2,1)S(1)}, bf16[2,4,4,48,1792]{4,3,2,1,0:T(8,128)(2,1)S(1)}, bf16[2,4,4,112,768]{4,3,2,1,0:T(8,128)(2,1...) custom-call(bf16[2,4,4,48,1792]{4,3,2,1,0:T(8,128)(2,1)} %bitcast.21, ...), custom_call_target="tpu_custom_call" | custom-call | tf_op jit(solution)/shard_map/pallas_call | solution.py:468
  82.1 6.1 %shard_map.188 = (bf16[2,4,4,48,1792]{4,3,2,1,0:T(8,128)(2,1)}, bf16[2,4,4,48,1792]{4,3,2,1,0:T(8,128)(2,1)}, bf16[2,4,4,112,768]{4,3,2,1,0:T(8,128)(2,1)}, f32[...) custom-call(bf16[2,4,4,48,1792]{4,3,2,1,0:T(8,128)(2,1)S(1)} %get-tu, ...), custom_call_target="tpu_custom_call" | custom-call | tf_op jit(solution)/shard_map/pallas_call | solution.py:477

commit v6 on v5

--- a/solution.py
+++ b/solution.py
@@ -14,15 +14,15 @@
 RP = (16, 16, 32)
 H = (6, 6, 14)
 AXES = ((0, 1, 2), (1, 2, 0), (2, 0, 1))
-TILES = ((1, 2, 2, 2), (1, 2, 2, 2), (1, 1, 1))
+TILES = ((1, 1, 1, 2, 2), (1, 1, 1, 2, 2), (1, 1, 1))
 VMEM_LIMIT = 49_500_000
 ORDER = (
-    "aaeeiibbfjeafbigdfejjcbhaieddkbgfgkihecacjbfikh",
-    "gedfbacijkhedgfcbakjhidgecbfkiahjedbeefcgaiikih",
-    "jeebbdcfgahjdikacffgbhjjjfkabaacccghikadeiegjfe",
-    "bbijjkahhcddhhkgggkdgcijffkachcdhfkdkdghjbckdg",
+    "aaffkkbggcahhflbddkgahljjedbalikhgejfmdkeighmcbcfdkamihl",
+    "bgedcfajhlkmiebgdajcfhilmkebcajdhfimkglaebachfjdgkhhikml",
+    "aafcekdajgibggklfmhhdjcgbigelflffmdglkhdjcaciimiemafbbmc",
+    "cllafgbjckkijeeemibibdddhecjjcjgkblldehfimmmejibclemj",
 )
-FIRST, PREPARE = 5, 30
+FIRST, PREPARE = 6, 34
 
 
 def adamw(w, m, v, g):
@@ -387,7 +387,7 @@
     stages = (st0, st1, st2, st3, st4, st5, st6, st7, st8, st9, st10, st11, st12, st13, st14, st15, st16)
     done = [0] * len(all_pairs)
     for n, letter in enumerate("".join(ORDER)):
-        p = "abcdefghijklmnop".index(letter)
+        p = ord(letter) - ord("a")
         stages[done[p]](all_pairs[p])
         done[p] += 1
         if n == PREPARE:

time: 88.3 us -> 88.9 us (level)
  no operation moved by 1% of the time
where the time goes in v6:
time: 88.9 us; the launch traced here: 88.8 us
  Pallas kernels  88.2 us (99%)
    pallas_call x1, Pallas kernels, step(): pl.pallas_call(comm_kernel, out_shape=[pltpu.VMEM(s, BF) for s in whole]...  82.1 us
    pallas_call x1, Pallas kernels, step(): pl.pallas_call(finish_kernel, out_shape=[jax.ShapeDtypeStruct(s, BF) for...  6.08 us

profile of v6, /device:TPU:1, one launch (start us, length us, event | category | flops | bytes accessed | tf_op | source)
XLA Modules:
  0.0 88.8 jit_solution(773260665748114020)
XLA Ops:
  0.6 82.1 %shard_map.187 = (bf16[2,4,4,48,1792]{4,3,2,1,0:T(8,128)(2,1)S(1)}, bf16[2,4,4,48,1792]{4,3,2,1,0:T(8,128)(2,1)S(1)}, bf16[2,4,4,112,768]{4,3,2,1,0:T(8,128)(2,1...) custom-call(bf16[2,4,4,48,1792]{4,3,2,1,0:T(8,128)(2,1)} %bitcast.21, ...), custom_call_target="tpu_custom_call" | custom-call | tf_op jit(solution)/shard_map/pallas_call | solution.py:468
  82.8 6.1 %shard_map.188 = (bf16[2,4,4,48,1792]{4,3,2,1,0:T(8,128)(2,1)}, bf16[2,4,4,48,1792]{4,3,2,1,0:T(8,128)(2,1)}, bf16[2,4,4,112,768]{4,3,2,1,0:T(8,128)(2,1)}, f32[...) custom-call(bf16[2,4,4,48,1792]{4,3,2,1,0:T(8,128)(2,1)S(1)} %get-tu, ...), custom_call_target="tpu_custom_call" | custom-call | tf_op jit(solution)/shard_map/pallas_call | solution.py:477
